TPU v7x, 32 devices: a whole 2x2x4 slice. The times are simulated.
32 devices in a mesh: dp: 4 (over y, x), block: 8 (over z, core).
Axes of the slice: x: 2, y: 2, z: 4, core: 2. Of those that a mesh axis runs over, the one named last changes fastest.
Arguments:
- grad_partial: float32 [4, 4, 8, 512, 512], P('dp', None, None, 'block'), may hold values from -6 to 6
- owner_table: int32 [4, 8], replicated, may hold values from 0 to 7, as said below
- left_factor: float32 [4, 8, 2, 512, 512], P('dp', 'block'), as said below
- right_factor: float32 [4, 8, 2, 512, 512], P('dp', 'block'), as said below
Outputs:
- update: bfloat16 [4, 8, 512, 512], P('dp', None, 'block')
- left_out: float32 [4, 8, 2, 512, 512], P('dp', 'block')
- right_out: float32 [4, 8, 2, 512, 512], P('dp', 'block')
Inputs may be any that keep to these rules, and one draw needn't show every extreme that they name: owner_table[d, j] is the owner of block (d, j); within each row d no owner appears more than 2 times, and some owner appears exactly 2 times. `left_factor`: each slot holds a symmetric positive definite matrix. `right_factor`: each slot holds a symmetric positive definite matrix.
All inputs are finite; a program needn't handle non-finite values.
Results may differ from a plain program's by a relative error of at most 0.0072.
Values may be sent and summed in bfloat16 or wider, within the bound.
No kernel may reach another device: no remote copies, remote signals or barrier semaphores. Data moves between devices by JAX's collectives and lax.ppermute only.
A program may use at most 128 MiB of HBM per device.

v0:
```python
import functools

import jax
import jax.numpy as jnp
from jax import lax
from jax.experimental import pallas as pl
from jax.experimental.pallas import tpu as pltpu
from jax.sharding import PartitionSpec as P

MOST = 2
POWER = 8

decay_rate = 0.9
damping = 0.1
epsilon = 1e-06

f32 = jnp.float32
bf16 = jnp.bfloat16
SMEM = pltpu.SMEM
VMEM = pltpu.VMEM
ANY = pl.ANY
LIMIT = 48 * 1024 * 1024


def mm(a, b):
    return jnp.dot(a, b, preferred_element_type=f32)


def arrange_kernel(scal, p_ref, a1_ref, b1_ref, a2_ref, b2_ref, *out_refs):
    count = p_ref.shape[1]
    cut = a2_ref.shape[-1]
    for slot, out_ref in enumerate(out_refs):

        def body(owner, carry, slot=slot, out_ref=out_ref):
            j = scal[3 + slot * count + owner]
            out_ref[owner, :, :cut] = (
                p_ref[0, j, :, :cut] + a1_ref[0, j].astype(f32) + a2_ref[j].astype(f32)
            ).astype(bf16)
            out_ref[owner, :, cut:] = (
                p_ref[0, j, :, cut:] + b1_ref[0, j].astype(f32) + b2_ref[j].astype(f32)
            ).astype(bf16)
            return carry

        lax.fori_loop(0, count, body, 0, unroll=count <= 8)


def arrange(scal, p, a1, b1, a2, b2):
    _, count, stripe, size = p.shape
    cut = size // 2
    out = jax.ShapeDtypeStruct((count, stripe, size), bf16)
    whole = lambda shape: pl.BlockSpec(shape, lambda i, s: (0,) * len(shape))
    return pl.pallas_call(
        arrange_kernel,
        grid_spec=pltpu.PrefetchScalarGridSpec(
            num_scalar_prefetch=1,
            grid=(1,),
            in_specs=[
                pl.BlockSpec((1, count, stripe, size), lambda i, s: (s[0], 0, 0, 0)),
                pl.BlockSpec((1, count, stripe, cut), lambda i, s: (s[1], 0, 0, 0)),
                pl.BlockSpec((1, count, stripe, cut), lambda i, s: (s[2], 0, 0, 0)),
                whole((count, stripe, cut)),
                whole((count, stripe, cut)),
            ],
            out_specs=[whole((count, stripe, size))] * MOST,
        ),
        out_shape=[out] * MOST,
        name="arrange",
    )(scal, p, a1, b1, a2, b2)


def place_kernel(scal, *refs):
    *in_refs, out_ref = refs
    count = out_ref.shape[0]

    def body(j, carry):
        owner = scal[j]
        rank = scal[count + j]
        value = in_refs[0][owner]
        for slot in range(1, MOST):
            value = jnp.where(rank == slot, in_refs[slot][owner], value)
        out_ref[j] = value
        return carry

    lax.fori_loop(0, count, body, 0, unroll=count <= 8)


def place(scal, returned):
    shape = returned[0].shape
    spec = pl.BlockSpec(memory_space=VMEM)
    return pl.pallas_call(
        place_kernel,
        in_specs=[pl.BlockSpec(memory_space=SMEM)] + [spec] * MOST,
        out_specs=spec,
        out_shape=jax.ShapeDtypeStruct(shape, bf16),
        name="place",
    )(scal, *returned)


def add_diagonal(ref, k, value):
    size = ref.shape[1]
    width = min(size, 128)
    rows = lax.broadcasted_iota(jnp.int32, (width, width), 0)
    columns = lax.broadcasted_iota(jnp.int32, (width, width), 1)
    spread = jnp.where(rows == columns, value, 0.0)
    for start in range(0, size, width):
        part = pl.ds(start, width)
        ref[k, part, part] += spread


def slot_kernel(slot, chained, active_ref, g_ref, l_hbm, r_hbm, *refs):
    refs = refs[2 * chained :]
    u_ref, lo_hbm, ro_hbm = refs[:3]
    s_ref, n_ref, *wides, y_ref, mb_narrow, tb_narrow, ub_ref, yb_ref, in_sem, out_sem = refs[3:]
    size = g_ref.shape[0]
    sides = (0, 1)
    states = (l_hbm, r_hbm)
    news = (lo_hbm, ro_hbm)
    loads = [pltpu.make_async_copy(states[k].at[slot], s_ref.at[k], in_sem.at[k]) for k in sides]
    stores = [pltpu.make_async_copy(n_ref.at[k], news[k].at[slot], out_sem.at[k]) for k in sides]
    for k in sides:
        loads[k].start()
    active = active_ref[slot] > 0

    @pl.when(active)
    def _():
        m_ref, t_ref = wides
        mb_ref, tb_ref = mb_narrow, tb_narrow
        g = g_ref[...]
        contract = ((1,), (0,))
        for k in sides:
            dims = ((contract[k], contract[k]), ((), ()))
            term = lax.dot_general(g, g, dims, preferred_element_type=f32)
            loads[k].wait()
            new = decay_rate * s_ref[k] + term * ((1.0 - decay_rate) / size)
            n_ref[k] = new
            m_ref[k] = new
            stores[k].start()
        for k in sides:
            add_diagonal(m_ref, k, jnp.full((1, 1), damping, f32))

        vectors = [jnp.full((1, size), size**-0.5, f32)] * 2
        lengths = [None, None]
        for turn in range(POWER):
            for k in sides:
                vectors[k] = jnp.sum(m_ref[k] * vectors[k], axis=1 - turn % 2, keepdims=True)
            for k in sides:
                square = jnp.sum(vectors[k] * vectors[k], axis=turn % 2, keepdims=True)
                lengths[k] = jnp.sqrt(square)
                vectors[k] = vectors[k] / lengths[k]

        scales = []
        for k in sides:
            ceiling = 1.25 * lengths[k]
            scales.append(lax.rsqrt(jnp.sqrt(ceiling)))
            scaled = m_ref[k] * (1.0 / ceiling)
            m_ref[k] = scaled
            mb_ref[k] = scaled.astype(bf16)
        for step in range(2):
            for k in sides:
                t = mm(mb_ref[k], mb_ref[k]) * (1 / 16) - 0.625 * m_ref[k]
                t_ref[k] = t
                tb_ref[k] = t.astype(bf16)
            for k in sides:
                ub_ref[k] = (3.125 * t_ref[k] + mm(tb_ref[k], tb_ref[k])).astype(bf16)
            for k in sides:
                t = (625 / 256) * m_ref[k] + mm(ub_ref[k], mb_ref[k])
                t_ref[k] = t
                tb_ref[k] = t.astype(bf16)
            if step == 0:
                for k in sides:
                    y = mm(mb_ref[k], tb_ref[k]) * (1 / 16) - 0.3125 * (m_ref[k] + t_ref[k])
                    y_ref[k] = y
                    yb_ref[k] = y.astype(bf16)
                m_ref, t_ref = t_ref, m_ref
                mb_ref, tb_ref = tb_ref, mb_ref
        for k in sides:
            x = 1.25 * y_ref[k] - (25 / 64) * t_ref[k] - 0.25 * mm(yb_ref[k], tb_ref[k])
            m_ref[k] = x * scales[k]
            add_diagonal(m_ref, k, (125 / 64) * scales[k])
            mb_ref[k] = m_ref[k].astype(bf16)

        mb_ref[0] = mm(mb_ref[0], g).astype(bf16)
        shaped = mm(mb_ref[0], mb_ref[1])
        m_ref[0] = shaped
        wide = g.astype(f32)
        count = size * size
        top = jnp.sum(jnp.sum(wide * wide, axis=0, keepdims=True), axis=1, keepdims=True) / count
        bottom = jnp.sum(jnp.sum(shaped * shaped, axis=0, keepdims=True), axis=1, keepdims=True) / count
        u_ref[...] = (m_ref[0] * (jnp.sqrt(top) / jnp.sqrt(bottom + epsilon))).astype(bf16)

    @pl.when(jnp.logical_not(active))
    def _():
        for k in sides:
            loads[k].wait()
            n_ref[k] = s_ref[k]
            stores[k].start()
        u_ref[...] = jnp.zeros_like(u_ref)

    for k in sides:
        stores[k].wait()


def run_slot(slot, active, g, left, right, chain):
    size = g.shape[-1]
    any_spec = pl.BlockSpec(memory_space=ANY)
    vmem_spec = pl.BlockSpec(memory_space=VMEM)
    wide = pltpu.VMEM((2, size, size), f32)
    narrow = pltpu.VMEM((2, size, size), bf16)
    chained = len(chain) // 2
    return pl.pallas_call(
        functools.partial(slot_kernel, slot, chained),
        in_specs=[pl.BlockSpec(memory_space=SMEM), vmem_spec, any_spec, any_spec]
        + [any_spec] * len(chain),
        out_specs=[vmem_spec, any_spec, any_spec],
        out_shape=[
            jax.ShapeDtypeStruct((size, size), bf16),
            jax.ShapeDtypeStruct(left.shape, f32),
            jax.ShapeDtypeStruct(right.shape, f32),
        ],
        scratch_shapes=[wide] * 5
        + [narrow] * 4
        + [pltpu.SemaphoreType.DMA((2,)), pltpu.SemaphoreType.DMA((2,))],
        input_output_aliases={4: 1, 5: 2} if chained else {},
        compiler_params=pltpu.CompilerParams(vmem_limit_bytes=LIMIT),
        cost_estimate=pl.CostEstimate(
            flops=40 * size**3, bytes_accessed=18 * size**2, transcendentals=0
        ),
        name=f"slot{slot}",
    )(active, g, left, right, *chain)


def tables(table_row, owner_index, count):
    order = jnp.arange(count, dtype=jnp.int32)
    earlier = order[:, None] < order[None, :]
    matching = table_row[:, None] == table_row[None, :]
    rank = jnp.sum(jnp.logical_and(matching, earlier), axis=0).astype(jnp.int32)
    slots = jnp.arange(MOST, dtype=jnp.int32)
    chooser = jnp.logical_and(
        table_row[None, None, :] == order[None, :, None],
        rank[None, None, :] == slots[:, None, None],
    )
    block_of = jnp.sum(jnp.where(chooser, order, 0), axis=2).astype(jnp.int32)
    mine = jnp.logical_and(table_row[None, :] == owner_index, rank[None, :] == slots[:, None])
    active = jnp.sum(mine, axis=1).astype(jnp.int32)
    return block_of.reshape(-1), rank, active


def local(grad_partial, owner_table, left_factor, right_factor):
    p = grad_partial[0]
    rows, count, stripe, size = p.shape
    data_index = lax.axis_index("dp")
    owner_index = lax.axis_index("block")
    table_row = lax.dynamic_index_in_dim(owner_table, data_index, 0, keepdims=False)
    block_of, rank, active = tables(table_row, owner_index, count)

    low, high = data_index % 2, data_index // 2
    cut = size // 2
    half_a = p[..., :cut].reshape(2, 2, count, stripe, cut)
    half_b = p[..., cut:].reshape(2, 2, count, stripe, cut)
    over_low = [(i, i ^ 1) for i in range(rows)]
    over_high = [(i, i ^ 2) for i in range(rows)]
    pick = functools.partial(lax.dynamic_index_in_dim, keepdims=False)
    a1 = lax.ppermute(pick(half_a, 1 - low, 1).astype(bf16), "dp", over_low)
    b1 = lax.ppermute(pick(half_b, 1 - high, 0).astype(bf16), "dp", over_high)
    a2 = pick(pick(half_a, 1 - high, 0), low, 0) + pick(a1, 1 - high, 0).astype(f32)
    a2 = lax.ppermute(a2.astype(bf16), "dp", over_high)
    b2 = pick(pick(half_b, high, 0), 1 - low, 0) + pick(b1, 1 - low, 0).astype(f32)
    b2 = lax.ppermute(b2.astype(bf16), "dp", over_low)
    scal = jnp.concatenate([jnp.stack([data_index, high, low]).astype(jnp.int32), block_of])
    outgoing = arrange(scal, p, a1, b1, a2, b2)

    left, right = left_factor[0, 0], right_factor[0, 0]
    received = [lax.all_to_all(out, "block", 0, 0, tiled=True) for out in outgoing]
    chain = ()
    returned = []
    for slot in range(MOST):
        update, *chain = run_slot(
            slot, active, received[slot].reshape(size, size), left, right, tuple(chain)
        )
        returned.append(
            lax.all_to_all(update.reshape(count, stripe, size), "block", 0, 0, tiled=True)
        )
    placed = place(jnp.concatenate([table_row, rank]), returned)
    new_left, new_right = chain
    return placed[None], new_left[None, None], new_right[None, None]


def solution(mesh):
    placed = (
        P("dp", None, None, "block", None),
        P(),
        P("dp", "block", None, None, None),
        P("dp", "block", None, None, None),
    )
    return jax.shard_map(
        local,
        mesh=mesh,
        in_specs=placed,
        out_specs=(
            P("dp", None, "block", None),
            P("dp", "block", None, None, None),
            P("dp", "block", None, None, None),
        ),
        check_vma=False,
    )
```

profile of v0, /device:TPU:0, one launch (start us, length us, event | category | flops | bytes accessed | tf_op | source)
XLA Modules:
  0.0 117.0 jit_solution(2286628522275774788)
XLA Ops:
  0.6 3.9 %fusion.7 = (f32[4,8,64,256]{3,2,1,0:T(8,128)}, f32[4,8,64,256]{3,2,1,0:T(8,128)S(1)}) fusion(f32[4,8,64,512]{3,2,1,0:T(8,128)} %bitcast.43), kind=kLoop, calls=%fused_computation.21 | loop fusion | bytes 8388608 | tf_op jit(solution)/shard_map/slice | solution.py:259
  4.6 2.1 %fusion = bf16[2,8,64,256]{3,2,1,0:T(8,128)(2,1)} fusion(f32[2,2,8,64,256]{4,3,2,1,0:T(8,128)} %bitcast.47, s32[]{:T(128)S(6)} %select_n.52), kind=kLoop, calls=%fused_computation.2 | loop fusion | bytes 1048580 | tf_op jit(solution)/shard_map/convert_element_type | solution.py:264
  6.7 3.0 %collective-permute-start.1 = (bf16[2,8,64,256]{3,2,1,0:T(8,128)(2,1)}, bf16[2,8,64,256]{3,2,1,0:T(8,128)(2,1)S(1)}, u32[]{:S(2)}, u32[]{:S(2)}) collective-permute-start(bf16[2,8,64,256]{3,2,1,0:T(8,128)(2,1)} %fusion), channel_id=1, source_target_pairs={{0,16},{8,24},{16,0},{24,8},{1,17},{9,25},{17,1},{25,9},{2,18},{10... | collective-permute-start | bytes 1572872 | tf_op jit(solution)/shard_map/ppermute | solution.py:264
  9.7 0.9 fusion.1
  10.5 1.5 %collective-permute-start = (bf16[2,8,64,256]{3,2,1,0:T(8,128)(2,1)}, bf16[2,8,64,256]{3,2,1,0:T(8,128)(2,1)S(1)}, u32[]{:S(2)}, u32[]{:S(2)}) collective-permute-start(bf16[2,8,64,256]{3,2,1,0:T(8,128)(2,1)} %fusion.1), channel_id=1, source_target_pairs={{0,8},{8,0},{16,24},{24,16},{1,9},{9,1},{17,25},{25,17},{2,10},{10... | collective-permute-start | bytes 1572872 | tf_op jit(solution)/shard_map/ppermute | solution.py:263
  12.0 0.1 convert_reduce_fusion
  12.1 9.7 %collective-permute-done.1.b1_ref = bf16[2,8,64,256]{3,2,1,0:T(8,128)(2,1)S(1)} collective-permute-done((bf16[2,8,64,256]{3,2,1,0:T(8,128)(2,1)}, bf16[2,8,64,256]{3,2,1,0:T(8,128)(2,1)S(1)}, u32[]{:S(2)}, u32[]{:S(2)}) %collective-permute-start.1) | collective-permute-done | bytes 524320 | tf_op jit(solution)/shard_map/ppermute | solution.py:264
  21.8 2.0 %fusion.2 = bf16[8,64,256]{2,1,0:T(8,128)(2,1)} fusion(f32[2,2,8,64,256]{4,3,2,1,0:T(8,128)} %bitcast.48, s32[]{:T(128)S(6)} %select_n.57, s32[]{:T(128)S(6)} %select_n.58, bf16[2,8,64,256]{3,2,1,0:T(8,128)(2,1)S(1)} %collective-permute-done.1.b1_ref, s32[]{:T(128)S(6)} %select_n.51), kind=kLoop, calls=%fused_computation.5 | loop fusion | flops 393216 | bytes 1048588 | tf_op jit(solution)/shard_map/convert_element_type | solution.py:268
  23.8 1.7 %collective-permute-start.3 = (bf16[8,64,256]{2,1,0:T(8,128)(2,1)}, bf16[8,64,256]{2,1,0:T(8,128)(2,1)S(1)}, u32[]{:S(2)}, u32[]{:S(2)}) collective-permute-start(bf16[8,64,256]{2,1,0:T(8,128)(2,1)} %fusion.2), channel_id=1, source_target_pairs={{0,8},{8,0},{16,24},{24,16},{1,9},{9,1},{17,25},{25,17},{2,10},{10... | collective-permute-start | bytes 786440 | tf_op jit(solution)/shard_map/ppermute | solution.py:268
  25.5 0.8 fusion.3
  26.4 1.5 %collective-permute-start.2 = (bf16[8,64,256]{2,1,0:T(8,128)(2,1)}, bf16[8,64,256]{2,1,0:T(8,128)(2,1)S(1)}, u32[]{:S(2)}, u32[]{:S(2)}) collective-permute-start(bf16[8,64,256]{2,1,0:T(8,128)(2,1)} %fusion.3), channel_id=1, source_target_pairs={{0,16},{8,24},{16,0},{24,8},{1,17},{9,25},{17,1},{25,9},{2,18},{10... | collective-permute-start | bytes 786440 | tf_op jit(solution)/shard_map/ppermute | solution.py:266
  27.9 0.1 select_reduce_fusion
  28.1 0.6 pad_add_fusion.1.scal
  28.8 2.7 %collective-permute-done.3.b2_ref = bf16[8,64,256]{2,1,0:T(8,128)(2,1)S(1)} collective-permute-done((bf16[8,64,256]{2,1,0:T(8,128)(2,1)}, bf16[8,64,256]{2,1,0:T(8,128)(2,1)S(1)}, u32[]{:S(2)}, u32[]{:S(2)}) %collective-permute-start.3) | collective-permute-done | bytes 262176 | tf_op jit(solution)/shard_map/ppermute | solution.py:268
  31.5 2.0 %collective-permute-done.2.a2_ref = bf16[8,64,256]{2,1,0:T(8,128)(2,1)S(1)} collective-permute-done((bf16[8,64,256]{2,1,0:T(8,128)(2,1)}, bf16[8,64,256]{2,1,0:T(8,128)(2,1)S(1)}, u32[]{:S(2)}, u32[]{:S(2)}) %collective-permute-start.2) | collective-permute-done | bytes 262176 | tf_op jit(solution)/shard_map/ppermute | solution.py:266
  33.5 0.7 copy-done.8
  34.2 3.4 %arrange.1 = (bf16[8,64,512]{2,1,0:T(8,128)(2,1)}, bf16[8,64,512]{2,1,0:T(8,128)(2,1)}) custom-call(s32[19]{0:T(128)} %pad_add_fusion.1.scal, f32[4,8,64,512]{3,2,1,0:T(8,128)} %bitcast.44, bf16[2,8,64,256]{3,2,1,0:T(8,128)(2,1)} %copy-done.6, bf16[2,8,64,256]{3,2,1,0:T(8,128)(2,1)} %copy-done.5, bf16[8,64,256]{2,1,0:T(8,128)(2,1)} %copy-done.8, ...), custom_call_target="tpu_custom_call" | custom-call | tf_op jit(solution)/shard_map/arrange/pallas_call | solution.py:52
  37.6 20.3 %all_to_all.20 = bf16[8,64,512]{2,1,0:T(8,128)(2,1)S(1)} all-to-all(bf16[8,64,512]{2,1,0:T(8,128)(2,1)} %get-tuple-element.11), channel_id=1, replica_groups=mesh['dp'=4,'block'=8] {'block'}, dimensions={0} | all-to-all | bytes 1048576 | tf_op jit(solution)/shard_map/all_to_all | solution.py:273
  57.9 3.5 %all-to-all-start.2 = ((bf16[8,64,512]{2,1,0:T(8,128)(2,1)}), bf16[8,64,512]{2,1,0:T(8,128)(2,1)S(1)}, u32[]{:S(2)}, u32[]{:S(2)}) async-start(bf16[8,64,512]{2,1,0:T(8,128)(2,1)} %get-tuple-element.13), calls=%async_computation.2 | async-start | bytes 1048576 | tf_op jit(solution)/shard_map/all_to_all | solution.py:273
  61.4 0.1 fusion.5.active_ref
  61.6 1.6 %copy-done.1 = f32[1,1,2,512,512]{4,3,2,1,0:T(8,128)S(1)} copy-done((f32[1,1,2,512,512]{4,3,2,1,0:T(8,128)S(1)}, f32[1,1,2,512,512]{4,3,2,1,0:T(8,128)}, u32[]{:S(2)}) %copy-start.1) | copy-done | bytes 2097176
  63.2 10.8 %slot0.1 = (bf16[512,512]{1,0:T(8,128)(2,1)}, f32[2,512,512]{2,1,0:T(8,128)}, f32[2,512,512]{2,1,0:T(8,128)}) custom-call(s32[2]{0:T(128)S(1)} %fusion.5.active_ref, bf16[512,512]{1,0:T(8,128)(2,1)S(1)} %bitcast.38, f32[2,512,512]{2,1,0:T(8,128)S(1)} %bitcast.39, f32[2,512,512]{2,1,0:T(8,128)S(1)} %bitcast.41), custom_call_target="tpu_custom_call" | custom-call | flops 5368709120 | bytes 4718592 | tf_op jit(solution)/shard_map/slot0/pallas_call | solution.py:210
  73.9 2.7 %all-to-all-done.2 = bf16[8,64,512]{2,1,0:T(8,128)(2,1)S(1)} async-done(((bf16[8,64,512]{2,1,0:T(8,128)(2,1)}), bf16[8,64,512]{2,1,0:T(8,128)(2,1)S(1)}, u32[]{:S(2)}, u32[]{:S(2)}) %all-to-all-start.2) | async-done | bytes 524320 | tf_op jit(solution)/shard_map/all_to_all | solution.py:273
  76.7 3.5 %all-to-all-start.1 = ((bf16[8,64,512]{2,1,0:T(8,128)(2,1)}), bf16[8,64,512]{2,1,0:T(8,128)(2,1)S(1)}, u32[]{:S(2)}, u32[]{:S(2)}) async-start(bf16[8,64,512]{2,1,0:T(8,128)(2,1)} %bitcast.17), calls=%async_computation.1 | async-start | bytes 1048576 | tf_op jit(solution)/shard_map/all_to_all | solution.py:281
  80.2 1.6 %copy-done.2 = f32[1,1,2,512,512]{4,3,2,1,0:T(8,128)S(1)} copy-done((f32[1,1,2,512,512]{4,3,2,1,0:T(8,128)S(1)}, f32[1,1,2,512,512]{4,3,2,1,0:T(8,128)}, u32[]{:S(2)}) %copy-start.2) | copy-done | bytes 2097176
  81.8 3.1 %slot1.1 = (bf16[512,512]{1,0:T(8,128)(2,1)}, f32[2,512,512]{2,1,0:T(8,128)}, f32[2,512,512]{2,1,0:T(8,128)}) custom-call(s32[2]{0:T(128)S(1)} %fusion.5.active_ref, bf16[512,512]{1,0:T(8,128)(2,1)S(1)} %bitcast.37, f32[2,512,512]{2,1,0:T(8,128)S(1)} %bitcast.40, f32[2,512,512]{2,1,0:T(8,128)S(1)} %bitcast.42, ...), custom_call_target="tpu_custom_call", output_to_operand_aliasing={{1}: (4, {}), {2}: (5, {})} | custom-call | flops 5368709120 | bytes 4718592 | tf_op jit(solution)/shard_map/slot1/pallas_call | solution.py:210
  84.9 10.6 %all-to-all-done.1.refs_0_ = bf16[8,64,512]{2,1,0:T(8,128)(2,1)S(1)} async-done(((bf16[8,64,512]{2,1,0:T(8,128)(2,1)}), bf16[8,64,512]{2,1,0:T(8,128)(2,1)S(1)}, u32[]{:S(2)}, u32[]{:S(2)}) %all-to-all-start.1) | async-done | bytes 524320 | tf_op jit(solution)/shard_map/all_to_all | solution.py:281
  95.4 3.5 %all-to-all-start.3 = ((bf16[8,64,512]{2,1,0:T(8,128)(2,1)}), bf16[8,64,512]{2,1,0:T(8,128)(2,1)S(1)}, u32[]{:S(2)}, u32[]{:S(2)}) async-start(bf16[8,64,512]{2,1,0:T(8,128)(2,1)} %bitcast.19), calls=%async_computation.3 | async-start | bytes 1048576 | tf_op jit(solution)/shard_map/all_to_all | solution.py:281
  98.9 0.6 pad_add_fusion.scal
  99.5 14.6 %all-to-all-done.3.refs_1_ = bf16[8,64,512]{2,1,0:T(8,128)(2,1)S(1)} async-done(((bf16[8,64,512]{2,1,0:T(8,128)(2,1)}), bf16[8,64,512]{2,1,0:T(8,128)(2,1)S(1)}, u32[]{:S(2)}, u32[]{:S(2)}) %all-to-all-start.3) | async-done | bytes 524320 | tf_op jit(solution)/shard_map/all_to_all | solution.py:281
  114.2 0.8 copy-done.4
  115.0 2.1 %place.1 = bf16[8,64,512]{2,1,0:T(8,128)(2,1)} custom-call(s32[16]{0:T(128)} %pad_add_fusion.scal, bf16[8,64,512]{2,1,0:T(8,128)(2,1)} %copy-done.3, bf16[8,64,512]{2,1,0:T(8,128)(2,1)} %copy-done.4), custom_call_target="tpu_custom_call" | custom-call | tf_op jit(solution)/shard_map/place/pallas_call | solution.py:90
  (22 shorter events, 0.2 us)
Async XLA Ops:
  4.6 7.4 %copy-start.9 = (s32[4,8]{1,0:T(4,128)S(1)}, s32[4,8]{1,0:T(4,128)}, u32[]{:S(2)}) copy-start(s32[4,8]{1,0:T(4,128)} %param.5) | copy-start | bytes 388
  6.7 15.1 %collective-permute-start.1 = (bf16[2,8,64,256]{3,2,1,0:T(8,128)(2,1)}, bf16[2,8,64,256]{3,2,1,0:T(8,128)(2,1)S(1)}, u32[]{:S(2)}, u32[]{:S(2)}) collective-permute-start(bf16[2,8,64,256]{3,2,1,0:T(8,128)(2,1)} %fusion), channel_id=1, source_target_pairs={{0,16},{8,24},{16,0},{24,8},{1,17},{9,25},{17,1},{25,9},{2,18},{10... | collective-permute-start | bytes 1572872 | tf_op jit(solution)/shard_map/ppermute | solution.py:264
  10.5 15.0 %collective-permute-start = (bf16[2,8,64,256]{3,2,1,0:T(8,128)(2,1)}, bf16[2,8,64,256]{3,2,1,0:T(8,128)(2,1)S(1)}, u32[]{:S(2)}, u32[]{:S(2)}) collective-permute-start(bf16[2,8,64,256]{3,2,1,0:T(8,128)(2,1)} %fusion.1), channel_id=1, source_target_pairs={{0,8},{8,0},{16,24},{24,16},{1,9},{9,1},{17,25},{25,17},{2,10},{10... | collective-permute-start | bytes 1572872 | tf_op jit(solution)/shard_map/ppermute | solution.py:263
  21.8 11.7 %copy-start.5 = (bf16[2,8,64,256]{3,2,1,0:T(8,128)(2,1)}, bf16[2,8,64,256]{3,2,1,0:T(8,128)(2,1)S(1)}, u32[]{:S(2)}) copy-start(bf16[2,8,64,256]{3,2,1,0:T(8,128)(2,1)S(1)} %collective-permute-done.1.b1_ref) | copy-start | bytes 1572868
  23.8 7.7 %collective-permute-start.3 = (bf16[8,64,256]{2,1,0:T(8,128)(2,1)}, bf16[8,64,256]{2,1,0:T(8,128)(2,1)S(1)}, u32[]{:S(2)}, u32[]{:S(2)}) collective-permute-start(bf16[8,64,256]{2,1,0:T(8,128)(2,1)} %fusion.2), channel_id=1, source_target_pairs={{0,8},{8,0},{16,24},{24,16},{1,9},{9,1},{17,25},{25,17},{2,10},{10... | collective-permute-start | bytes 786440 | tf_op jit(solution)/shard_map/ppermute | solution.py:268
  25.5 8.0 %copy-start.6 = (bf16[2,8,64,256]{3,2,1,0:T(8,128)(2,1)}, bf16[2,8,64,256]{3,2,1,0:T(8,128)(2,1)S(1)}, u32[]{:S(2)}) copy-start(bf16[2,8,64,256]{3,2,1,0:T(8,128)(2,1)S(1)} %collective-permute-done.a1_ref) | copy-start | bytes 1572868
  26.4 7.1 %collective-permute-start.2 = (bf16[8,64,256]{2,1,0:T(8,128)(2,1)}, bf16[8,64,256]{2,1,0:T(8,128)(2,1)S(1)}, u32[]{:S(2)}, u32[]{:S(2)}) collective-permute-start(bf16[8,64,256]{2,1,0:T(8,128)(2,1)} %fusion.3), channel_id=1, source_target_pairs={{0,16},{8,24},{16,0},{24,8},{1,17},{9,25},{17,1},{25,9},{2,18},{10... | collective-permute-start | bytes 786440 | tf_op jit(solution)/shard_map/ppermute | solution.py:266
  31.5 2.0 %copy-start.7 = (bf16[8,64,256]{2,1,0:T(8,128)(2,1)}, bf16[8,64,256]{2,1,0:T(8,128)(2,1)S(1)}, u32[]{:S(2)}) copy-start(bf16[8,64,256]{2,1,0:T(8,128)(2,1)S(1)} %collective-permute-done.3.b2_ref) | copy-start | bytes 786436
  33.5 0.7 copy-start.8
  37.6 24.0 %copy-start = (f32[1,1,2,512,512]{4,3,2,1,0:T(8,128)S(1)}, f32[1,1,2,512,512]{4,3,2,1,0:T(8,128)}, u32[]{:S(2)}) copy-start(f32[1,1,2,512,512]{4,3,2,1,0:T(8,128)} %param.6) | copy-start | bytes 6291460
  57.9 18.8 %all-to-all-start.2 = ((bf16[8,64,512]{2,1,0:T(8,128)(2,1)}), bf16[8,64,512]{2,1,0:T(8,128)(2,1)S(1)}, u32[]{:S(2)}, u32[]{:S(2)}) async-start(bf16[8,64,512]{2,1,0:T(8,128)(2,1)} %get-tuple-element.13), calls=%async_computation.2 | async-start | bytes 1048576 | tf_op jit(solution)/shard_map/all_to_all | solution.py:273
  61.6 1.6 %copy-start.1 = (f32[1,1,2,512,512]{4,3,2,1,0:T(8,128)S(1)}, f32[1,1,2,512,512]{4,3,2,1,0:T(8,128)}, u32[]{:S(2)}) copy-start(f32[1,1,2,512,512]{4,3,2,1,0:T(8,128)} %param.7) | copy-start | bytes 6291460
  76.7 18.8 %all-to-all-start.1 = ((bf16[8,64,512]{2,1,0:T(8,128)(2,1)}), bf16[8,64,512]{2,1,0:T(8,128)(2,1)S(1)}, u32[]{:S(2)}, u32[]{:S(2)}) async-start(bf16[8,64,512]{2,1,0:T(8,128)(2,1)} %bitcast.17), calls=%async_computation.1 | async-start | bytes 1048576 | tf_op jit(solution)/shard_map/all_to_all | solution.py:281
  80.2 1.6 %copy-start.2 = (f32[1,1,2,512,512]{4,3,2,1,0:T(8,128)S(1)}, f32[1,1,2,512,512]{4,3,2,1,0:T(8,128)}, u32[]{:S(2)}) copy-start(f32[1,1,2,512,512]{4,3,2,1,0:T(8,128)} %param.7) | copy-start | bytes 6291460
  95.4 18.8 %copy-start.3 = (bf16[8,64,512]{2,1,0:T(8,128)(2,1)}, bf16[8,64,512]{2,1,0:T(8,128)(2,1)S(1)}, u32[]{:S(2)}) copy-start(bf16[8,64,512]{2,1,0:T(8,128)(2,1)S(1)} %all-to-all-done.1.refs_0_) | copy-start | bytes 1572868
  95.4 18.8 %all-to-all-start.3 = ((bf16[8,64,512]{2,1,0:T(8,128)(2,1)}), bf16[8,64,512]{2,1,0:T(8,128)(2,1)S(1)}, u32[]{:S(2)}, u32[]{:S(2)}) async-start(bf16[8,64,512]{2,1,0:T(8,128)(2,1)} %bitcast.19), calls=%async_computation.3 | async-start | bytes 1048576 | tf_op jit(solution)/shard_map/all_to_all | solution.py:281
  114.2 0.8 copy-start.4
where the time goes:
time: 118 us; the launch traced here: 117 us
  waiting for transfers between devices  42.4 us (36%)
  blocking collectives  20.3 us (17%)
  Pallas kernels  19.3 us (16%)
  starting transfers between devices  18.2 us (15%)
  local copies, waits for them, and re-layouts  11.7 us (10%)
  other arithmetic  4.46 us (4%)
    all_to_all x2, waiting for transfers between devices, local(): lax.all_to_all(update.reshape(count, stripe, size), 'block', 0, 0, tiled=...  25.2 us
    all_to_all x1, blocking collectives, local(): lax.all_to_all(out, 'block', 0, 0, tiled=True)  20.3 us
    pallas_call x2, Pallas kernels, run_slot(): pl.pallas_call(functools.partial(slot_kernel, slot, chained), in_specs=[p...  13.8 us
    ppermute x1, waiting for transfers between devices, local(): b1 = lax.ppermute(pick(half_b, 1 - high, 0).astype(bf16), 'dp', over_high)  9.68 us
    all_to_all x2, starting transfers between devices, local(): lax.all_to_all(update.reshape(count, stripe, size), 'block', 0, 0, tiled=...  6.99 us
    unnamed x20, local copies, waits for them, and re-layouts  4.7 us
    slice x1, local copies, waits for them, and re-layouts, local(): half_b = p[..., cut:].reshape(2, 2, count, stripe, cut)  3.94 us
    all_to_all x1, starting transfers between devices, local(): lax.all_to_all(out, 'block', 0, 0, tiled=True)  3.49 us
  transfers between devices with their start and end apart: 7, of which 6 were waited for; matrix products, arithmetic and copies ran while one was open for 5% of the time, Pallas kernels for 12%

commit v1 on v0

v1 whole, which is shorter than its diff:
```python
import functools

import jax
import jax.numpy as jnp
from jax import lax
from jax.experimental import pallas as pl
from jax.experimental.pallas import tpu as pltpu
from jax.sharding import PartitionSpec as P


MOST = 2
POWER = 8

decay_rate = 0.9
damping = 0.1
epsilon = 1e-06

f32 = jnp.float32
bf16 = jnp.bfloat16
SMEM = pltpu.SMEM
VMEM = pltpu.VMEM
ANY = pltpu.HBM
LIMIT = 24 * 1024 * 1024
SMALL = 8 * 1024 * 1024


def mm(a, b):
    return jnp.dot(a, b, preferred_element_type=f32)


def call(kernel, out_shape, scratch, operands, flops=0, aliases={}, limit=SMALL):
    outs = [shape for shape, _ in out_shape]
    size = sum(array.size * array.dtype.itemsize for array, _ in operands)
    return pl.pallas_call(
        kernel,
        in_specs=[pl.BlockSpec(memory_space=space) for _, space in operands],
        out_specs=[pl.BlockSpec(memory_space=space) for _, space in out_shape],
        out_shape=outs,
        scratch_shapes=scratch,
        input_output_aliases=aliases,
        compiler_params=pltpu.CompilerParams(vmem_limit_bytes=limit),
        cost_estimate=pl.CostEstimate(flops=flops, bytes_accessed=size, transcendentals=0),
    )(*[array for array, _ in operands])


def cast_kernel(scal, p_ref, a_ref, b_ref):
    cut = a_ref.shape[-1]
    high, low = scal[0], scal[1]
    for other in range(2):
        a_ref[other] = p_ref[other, 1 - low, :, :, :cut].astype(bf16)
        b_ref[other] = p_ref[1 - high, other, :, :, cut:].astype(bf16)


def keep_kernel(scal, p_ref, a_ref, b_ref):
    cut = a_ref.shape[-1]
    high, low = scal[0], scal[1]
    a_ref[...] = p_ref[1 - high, low, :, :, :cut]
    b_ref[...] = p_ref[high, 1 - low, :, :, cut:]


def half_kernel(scal, p_ref, a1_ref, b1_ref, own_ref):
    cut = a1_ref.shape[-1]
    high, low = scal[0], scal[1]
    own_ref[:, :, :cut] = p_ref[high, low, :, :, :cut] + a1_ref[high].astype(f32)
    own_ref[:, :, cut:] = p_ref[high, low, :, :, cut:] + b1_ref[low].astype(f32)


def forward_kernel(scal, pa_ref, pb_ref, a1_ref, b1_ref, a_ref, b_ref):
    high, low = scal[0], scal[1]
    a_ref[...] = (pa_ref[...] + a1_ref[1 - high].astype(f32)).astype(bf16)
    b_ref[...] = (pb_ref[...] + b1_ref[1 - low].astype(f32)).astype(bf16)


def total_kernel(own_ref, a2_ref, b2_ref, out_ref):
    cut = a2_ref.shape[-1]
    out_ref[:, :, :cut] = (own_ref[:, :, :cut] + a2_ref[...].astype(f32)).astype(bf16)
    out_ref[:, :, cut:] = (own_ref[:, :, cut:] + b2_ref[...].astype(f32)).astype(bf16)


def sum_over_dp(grad_partial, scal):
    rows, count, stripe, size = grad_partial.shape
    p = grad_partial.reshape(2, rows // 2, count, stripe, size)
    over_low = [(i, i ^ 1) for i in range(rows)]
    over_high = [(i, i ^ 2) for i in range(rows)]
    shape = (count, stripe, size // 2)
    pair = (jax.ShapeDtypeStruct((2,) + shape, bf16), VMEM)
    one = (jax.ShapeDtypeStruct(shape, bf16), VMEM)
    both = (jax.ShapeDtypeStruct((count, stripe, size), bf16), VMEM)
    fixed = [(scal, SMEM), (p, VMEM)]
    a, b = call(cast_kernel, [pair] * 2, [], fixed)
    first = [lax.ppermute(a, "dp", over_low), lax.ppermute(b, "dp", over_high)]
    kept = [(jax.ShapeDtypeStruct(shape, f32), VMEM)] * 2
    pa, pb = call(keep_kernel, kept, [], fixed)
    arrived = [(array, VMEM) for array in first]
    operands = [(scal, SMEM), (pa, VMEM), (pb, VMEM)] + arrived
    a, b = call(forward_kernel, [one] * 2, [], operands)
    second = [lax.ppermute(a, "dp", over_high), lax.ppermute(b, "dp", over_low)]
    whole = [(jax.ShapeDtypeStruct((count, stripe, size), f32), VMEM)]
    (own,) = call(half_kernel, whole, [], fixed + arrived)
    operands = [(own, VMEM)] + [(array, VMEM) for array in second]
    (total,) = call(total_kernel, [both], [], operands)
    return total


def arrange_kernel(count, scal, own_ref, other_ref, *out_refs):
    me = scal[2]
    core, chip = me % 2, me // 2
    chips = count // 2
    for slot in range(MOST):
        for r in range(chips):
            j = scal[3 + slot * count + lax.bitwise_xor(chip, r) * 2 + core]
            out_ref = out_refs[slot * chips + r]
            out_ref[core] = own_ref[j]
            out_ref[1 - core] = other_ref[j]


def stage_kernel(l_ref, r_ref, l_out, r_out):
    l_out[...] = l_ref[...]
    r_out[...] = r_ref[...]


def give_kernel(scal, *refs):
    *in_refs, out_ref = refs
    core = scal[2] % 2
    for r, in_ref in enumerate(in_refs):
        out_ref[r] = in_ref[1 - core]


def place_kernel(count, scal, *refs):
    *in_refs, out_ref = refs
    me = scal[2]
    core, chip = me % 2, me // 2
    chips = count // 2
    pieces = []
    for r in range(chips):
        base = lax.bitwise_xor(chip, r) * 2
        pieces.append((base + core, in_refs[r], core))
        pieces.append((base + 1 - core, in_refs[chips], r))
    for q in range(count):
        pieces.append((count + lax.bitwise_xor(me, q), in_refs[chips + 1 + q], None))
    for entry, ref, index in pieces:
        at = 3 + entry

        @pl.when(scal[at + MOST * count] > 0)
        def _(at=at, ref=ref, index=index):
            out_ref[scal[at]] = ref[...] if index is None else ref[index]


def over_block(arrays, count, stride):
    return [arrays[0]] + [
        lax.ppermute(array, "block", [(i, i ^ (r * stride)) for i in range(count)])
        for r, array in enumerate(arrays)
        if r > 0
    ]


def add_diagonal(ref, k, value):
    size = ref.shape[1]
    width = min(size, 128)
    rows = lax.broadcasted_iota(jnp.int32, (width, width), 0)
    columns = lax.broadcasted_iota(jnp.int32, (width, width), 1)
    spread = jnp.where(rows == columns, value, 0.0)
    for start in range(0, size, width):
        part = pl.ds(start, width)
        ref[k, part, part] += spread


def slot_kernel(slot, direct, count, scal, l_ref, r_ref, *refs):
    chips = count // 2
    in_refs, refs = refs[:chips], refs[chips + (2 if slot else 0) :]
    n_out = count if direct else chips
    out_refs, refs = refs[:n_out], refs[n_out:]
    lo_hbm, ro_hbm, g_ref, n_ref, *wides, y_ref = refs[:7]
    mb_narrow, tb_narrow, ub_ref, yb_ref, out_sem = refs[7:]
    size = g_ref.shape[0]
    stripe = size // count
    me = scal[2]
    chip = me // 2
    sides = (0, 1)
    states = (l_ref, r_ref)
    news = (lo_hbm, ro_hbm)
    stores = [pltpu.make_async_copy(n_ref.at[k], news[k].at[slot], out_sem.at[k]) for k in sides]
    active = scal[3 + (MOST + slot) * count + me] > 0

    @pl.when(active)
    def _():
        m_ref, t_ref = wides
        mb_ref, tb_ref = mb_narrow, tb_narrow
        for r, ref in enumerate(in_refs):
            for c in range(2):
                start = pl.multiple_of((lax.bitwise_xor(chip, r) * 2 + c) * stripe, stripe)
                g_ref[pl.ds(start, stripe), :] = ref[c]
        g = g_ref[...]
        contract = ((1,), (0,))
        for k in sides:
            dims = ((contract[k], contract[k]), ((), ()))
            term = lax.dot_general(g, g, dims, preferred_element_type=f32)
            new = decay_rate * states[k][slot] + term * ((1.0 - decay_rate) / size)
            n_ref[k] = new
            m_ref[k] = new
            stores[k].start()
        for k in sides:
            add_diagonal(m_ref, k, jnp.full((1, 1), damping, f32))

        vectors = [jnp.full((1, size), size**-0.5, f32)] * 2
        lengths = [None, None]
        for turn in range(POWER):
            for k in sides:
                vectors[k] = jnp.sum(m_ref[k] * vectors[k], axis=1 - turn % 2, keepdims=True)
            for k in sides:
                square = jnp.sum(vectors[k] * vectors[k], axis=turn % 2, keepdims=True)
                lengths[k] = jnp.sqrt(square)
                vectors[k] = vectors[k] / lengths[k]

        scales = []
        for k in sides:
            ceiling = 1.25 * lengths[k]
            scales.append(lax.rsqrt(jnp.sqrt(ceiling)))
            scaled = m_ref[k] * (1.0 / ceiling)
            m_ref[k] = scaled
            mb_ref[k] = scaled.astype(bf16)
        for step in range(2):
            for k in sides:
                t = mm(mb_ref[k], mb_ref[k]) * (1 / 16) - 0.625 * m_ref[k]
                t_ref[k] = t
                tb_ref[k] = t.astype(bf16)
            for k in sides:
                ub_ref[k] = (3.125 * t_ref[k] + mm(tb_ref[k], tb_ref[k])).astype(bf16)
            for k in sides:
                t = (625 / 256) * m_ref[k] + mm(ub_ref[k], mb_ref[k])
                t_ref[k] = t
                tb_ref[k] = t.astype(bf16)
            if step == 0:
                for k in sides:
                    y = mm(mb_ref[k], tb_ref[k]) * (1 / 16) - 0.3125 * (m_ref[k] + t_ref[k])
                    y_ref[k] = y
                    yb_ref[k] = y.astype(bf16)
                m_ref, t_ref = t_ref, m_ref
                mb_ref, tb_ref = tb_ref, mb_ref
        for k in sides:
            x = 1.25 * y_ref[k] - (25 / 64) * t_ref[k] - 0.25 * mm(yb_ref[k], tb_ref[k])
            m_ref[k] = x * scales[k]
            add_diagonal(m_ref, k, (125 / 64) * scales[k])
            mb_ref[k] = m_ref[k].astype(bf16)

        mb_ref[0] = mm(mb_ref[0], g).astype(bf16)
        shaped = mm(mb_ref[0], mb_ref[1])
        m_ref[0] = shaped
        wide = g.astype(f32)
        entries = size * size
        top = jnp.sum(jnp.sum(wide * wide, axis=0, keepdims=True), axis=1, keepdims=True) / entries
        bottom = jnp.sum(jnp.sum(shaped * shaped, axis=0, keepdims=True), axis=1, keepdims=True) / entries
        scale = jnp.sqrt(top) / jnp.sqrt(bottom + epsilon)

        def rows_of(device):
            part = pl.ds(pl.multiple_of(device * stripe, stripe), stripe)
            return (m_ref[0, part, :] * scale).astype(bf16)

        if direct:
            for q in range(count):
                out_refs[q][...] = rows_of(lax.bitwise_xor(me, q))
        else:
            for r in range(chips):
                for c in range(2):
                    out_refs[r][c] = rows_of(lax.bitwise_xor(chip, r) * 2 + c)

    @pl.when(jnp.logical_not(active))
    def _():
        for k in sides:
            n_ref[k] = states[k][slot]
            stores[k].start()
        for out_ref in out_refs:
            out_ref[...] = jnp.zeros_like(out_ref)

    for k in sides:
        stores[k].wait()


def run_slot(slot, direct, scal, pieces, left, right, chain):
    size = left.shape[-1]
    stripe = pieces[0].shape[1]
    count = size // stripe
    wide = pltpu.VMEM((2, size, size), f32)
    narrow = pltpu.VMEM((2, size, size), bf16)
    sem = pltpu.SemaphoreType.DMA((2,))
    if direct:
        out = [(jax.ShapeDtypeStruct((stripe, size), bf16), VMEM)] * count
    else:
        out = [(jax.ShapeDtypeStruct((2, stripe, size), bf16), VMEM)] * (count // 2)
    news = [(jax.ShapeDtypeStruct(state.shape, f32), ANY) for state in (left, right)]
    operands = [(scal, SMEM), (left, VMEM), (right, VMEM)] + [(piece, VMEM) for piece in pieces]
    operands += [(state, ANY) for state in chain]
    aliases = {len(operands) - 2 + k: len(out) + k for k in range(2)} if chain else {}
    *updates, new_left, new_right = call(
        functools.partial(slot_kernel, slot, direct, count),
        out + news,
        [pltpu.VMEM((size, size), bf16)] + [wide] * 4 + [narrow] * 4 + [sem],
        operands,
        flops=40 * size**3,
        aliases=aliases,
        limit=LIMIT,
    )
    return updates, (new_left, new_right)


def tables(table_row, count):
    order = jnp.arange(count, dtype=jnp.int32)
    earlier = order[:, None] < order[None, :]
    matching = table_row[:, None] == table_row[None, :]
    rank = jnp.sum(jnp.logical_and(matching, earlier), axis=0).astype(jnp.int32)
    slots = jnp.arange(MOST, dtype=jnp.int32)
    chooser = jnp.logical_and(
        table_row[None, None, :] == order[None, :, None],
        rank[None, None, :] == slots[:, None, None],
    )
    block_of = jnp.sum(jnp.where(chooser, order, 0), axis=2).astype(jnp.int32)
    used = jnp.sum(chooser, axis=2).astype(jnp.int32)
    return jnp.concatenate([block_of.reshape(-1), used.reshape(-1)])


def step(grad_partial, owner_table, left_factor, right_factor):
    _, count, stripe, size = grad_partial.shape[1:]
    data_index = lax.axis_index("dp").astype(jnp.int32)
    owner_index = lax.axis_index("block").astype(jnp.int32)
    table_row = lax.dynamic_index_in_dim(owner_table, data_index, 0, keepdims=False)
    place_of = jnp.stack([data_index // 2, data_index % 2, owner_index])
    scal = jnp.concatenate([place_of, tables(table_row, count)])
    left, right = left_factor[0, 0], right_factor[0, 0]

    chips = count // 2
    cores = [(i, i ^ 1) for i in range(count)]
    total = sum_over_dp(grad_partial[0], place_of)
    other = lax.ppermute(total, "block", cores)
    message = (jax.ShapeDtypeStruct((2, stripe, size), bf16), VMEM)
    messages = call(
        functools.partial(arrange_kernel, count),
        [message] * (MOST * chips),
        [],
        [(scal, SMEM), (total, VMEM), (other, VMEM)],
    )
    pieces = []
    for slot in range(MOST):
        pieces.append(over_block(messages[slot * chips : (slot + 1) * chips], count, 2))

    states = [(state, VMEM) for state in (left, right)]
    kept = [(jax.ShapeDtypeStruct(left.shape, f32), VMEM)] * 2
    left, right = call(stage_kernel, kept, [], states)

    updates, chain = run_slot(0, False, scal, pieces[0], left, right, ())
    returned = over_block(updates, count, 2)
    updates, chain = run_slot(1, True, scal, pieces[1], left, right, chain)
    direct = over_block(updates, count, 1)
    (given,) = call(
        give_kernel,
        [(jax.ShapeDtypeStruct((chips, stripe, size), bf16), VMEM)],
        [],
        [(scal, SMEM)] + [(piece, VMEM) for piece in returned],
    )
    given = lax.ppermute(given, "block", cores)
    (placed,) = call(
        functools.partial(place_kernel, count),
        [(jax.ShapeDtypeStruct((count, stripe, size), bf16), VMEM)],
        [],
        [(scal, SMEM)] + [(piece, VMEM) for piece in returned + [given] + direct],
    )
    new_left, new_right = chain
    return placed[None], new_left[None, None], new_right[None, None]


def solution(mesh):
    placed = (
        P("dp", None, None, "block", None),
        P(),
        P("dp", "block", None, None, None),
        P("dp", "block", None, None, None),
    )
    return jax.shard_map(
        step,
        mesh=mesh,
        in_specs=placed,
        out_specs=(
            P("dp", None, "block", None),
            P("dp", "block", None, None, None),
            P("dp", "block", None, None, None),
        ),
        check_vma=False,
    )
```

time: 118 us -> 106 us (0.90)
  blocking collectives: 20.3 us -> 0 us
  starting transfers between devices: 18.2 us -> 27.9 us
  local copies, waits for them, and re-layouts: 11.7 us -> 6.23 us
  Pallas kernels: 19.3 us -> 23.9 us
  other arithmetic: 4.46 us -> 0.33 us
  waiting for transfers between devices: 42.4 us -> 46.3 us
    ppermute x4 -> x22, waiting for transfers between devices: 14.4 us -> 46.3 us  [the longest x16 30.4 us: over_block(): lax.ppermute(array, 'block', [(i, i ^ r * stride) for i in range(count)])]
    all_to_all x3 -> x0, waiting for transfers between devices: 27.9 us -> none  [the longest x2 25.2 us: local(): lax.all_to_all(update.reshape(count, stripe, size), 'block', 0, 0, tiled=...]
    all_to_all x1 -> x0, blocking collectives: 20.3 us -> none  [local(): lax.all_to_all(out, 'block', 0, 0, tiled=True)]
    ppermute x4 -> x22, starting transfers between devices: 7.72 us -> 27.9 us  [the longest x16 21 us: over_block(): lax.ppermute(array, 'block', [(i, i ^ r * stride) for i in range(count)])]
    all_to_all x3 -> x0, starting transfers between devices: 10.5 us -> none  [the longest x2 6.99 us: local(): lax.all_to_all(update.reshape(count, stripe, size), 'block', 0, 0, tiled=...]
    pallas_call x4 -> x11, Pallas kernels: 19.3 us -> 23.9 us  [call(): pl.pallas_call(kernel, in_specs=[pl.BlockSpec(memory_space=space) for _,...]
    slice x1 -> x0, local copies, waits for them, and re-layouts: 3.94 us -> none  [local(): half_b = p[..., cut:].reshape(2, 2, count, stripe, cut)]
    convert_element_type x2 -> x0, local copies, waits for them, and re-layouts: 2.95 us -> none  [the longest x1 2.1 us: local(): b1 = lax.ppermute(pick(half_b, 1 - high, 0).astype(bf16), 'dp', over_high)]
  transfers between devices with their start and end apart: 7 -> 22, of which waited for: 6 -> 14; matrix products, arithmetic and copies ran while one was open for 5% -> 0% of each run, Pallas kernels for 12% -> 11%
where the time goes in v1:
time: 106 us; the launch traced here: 105 us
  waiting for transfers between devices  46.3 us (44%)
  starting transfers between devices  27.9 us (26%)
  Pallas kernels  23.9 us (23%)
  local copies, waits for them, and re-layouts  6.23 us (6%)
    ppermute x16, waiting for transfers between devices, over_block(): lax.ppermute(array, 'block', [(i, i ^ r * stride) for i in range(count)])  30.4 us
    pallas_call x11, Pallas kernels, call(): pl.pallas_call(kernel, in_specs=[pl.BlockSpec(memory_space=space) for _,...  23.9 us
    ppermute x16, starting transfers between devices, over_block(): lax.ppermute(array, 'block', [(i, i ^ r * stride) for i in range(count)])  21 us
    ppermute x2, waiting for transfers between devices, sum_over_dp(): first = [lax.ppermute(a, 'dp', over_low), lax.ppermute(b, 'dp', over_high)]  11.2 us
    unnamed x10, local copies, waits for them, and re-layouts  5.98 us
    ppermute x2, starting transfers between devices, sum_over_dp(): first = [lax.ppermute(a, 'dp', over_low), lax.ppermute(b, 'dp', over_high)]  4.55 us
    ppermute x2, waiting for transfers between devices, sum_over_dp(): second = [lax.ppermute(a, 'dp', over_high), lax.ppermute(b, 'dp', over_low)]  3.16 us
  transfers between devices with their start and end apart: 22, of which 14 were waited for; matrix products, arithmetic and copies ran while one was open for 0% of the time, Pallas kernels for 11%

profile of v1, /device:TPU:0, one launch (start us, length us, event | category | flops | bytes accessed | tf_op | source)
XLA Modules:
  0.0 105.5 jit_solution(15714868374278401674)
XLA Ops:
  0.7 2.2 %copy-done.1 = f32[1,4,8,64,512]{4,3,2,1,0:T(8,128)S(1)} copy-done((f32[1,4,8,64,512]{4,3,2,1,0:T(8,128)S(1)}, f32[1,4,8,64,512]{4,3,2,1,0:T(8,128)}, u32[]{:S(2)}) %copy-start.1) | copy-done | bytes 4194328
  2.9 0.7 shard_map.68
  3.6 3.0 %collective-permute-start = (bf16[2,8,64,256]{3,2,1,0:T(8,128)(2,1)S(1)}, bf16[2,8,64,256]{3,2,1,0:T(8,128)(2,1)S(1)}, u32[]{:S(2)}, u32[]{:S(2)}) collective-permute-start(bf16[2,8,64,256]{3,2,1,0:T(8,128)(2,1)S(1)} %get-tuple-element.37), channel_id=1, source_target_pairs={{0,8},{8,0},{16,24},{24,16},{1,9},{9,1},{17,25},{25,17},{2,10},{10... | collective-permute-start | bytes 1572872 | tf_op jit(solution)/shard_map/ppermute | solution.py:91
  6.6 1.5 %collective-permute-start.1 = (bf16[2,8,64,256]{3,2,1,0:T(8,128)(2,1)S(1)}, bf16[2,8,64,256]{3,2,1,0:T(8,128)(2,1)S(1)}, u32[]{:S(2)}, u32[]{:S(2)}) collective-permute-start(bf16[2,8,64,256]{3,2,1,0:T(8,128)(2,1)S(1)} %get-tuple-element.38), channel_id=1, source_target_pairs={{0,16},{8,24},{16,0},{24,8},{1,17},{9,25},{17,1},{25,9},{2,18},{10... | collective-permute-start | bytes 1572872 | tf_op jit(solution)/shard_map/ppermute | solution.py:91
  8.8 9.8 %collective-permute-done.a1_ref = bf16[2,8,64,256]{3,2,1,0:T(8,128)(2,1)S(1)} collective-permute-done((bf16[2,8,64,256]{3,2,1,0:T(8,128)(2,1)S(1)}, bf16[2,8,64,256]{3,2,1,0:T(8,128)(2,1)S(1)}, u32[]{:S(2)}, u32[]{:S(2)}) %collective-permute-start) | collective-permute-done | bytes 524320 | tf_op jit(solution)/shard_map/ppermute | solution.py:91
  18.6 1.5 %collective-permute-done.1.b1_ref = bf16[2,8,64,256]{3,2,1,0:T(8,128)(2,1)S(1)} collective-permute-done((bf16[2,8,64,256]{3,2,1,0:T(8,128)(2,1)S(1)}, bf16[2,8,64,256]{3,2,1,0:T(8,128)(2,1)S(1)}, u32[]{:S(2)}, u32[]{:S(2)}) %collective-permute-start.1) | collective-permute-done | bytes 524320 | tf_op jit(solution)/shard_map/ppermute | solution.py:91
  20.0 0.6 shard_map.71
  20.7 1.6 %collective-permute-start.2 = (bf16[8,64,256]{2,1,0:T(8,128)(2,1)S(1)}, bf16[8,64,256]{2,1,0:T(8,128)(2,1)S(1)}, u32[]{:S(2)}, u32[]{:S(2)}) collective-permute-start(bf16[8,64,256]{2,1,0:T(8,128)(2,1)S(1)} %get-tuple-element.41), channel_id=1, source_target_pairs={{0,16},{8,24},{16,0},{24,8},{1,17},{9,25},{17,1},{25,9},{2,18},{10... | collective-permute-start | bytes 786440 | tf_op jit(solution)/shard_map/ppermute | solution.py:97
  22.9 2.2 %copy-done.2 = f32[1,4,8,64,512]{4,3,2,1,0:T(8,128)S(1)} copy-done((f32[1,4,8,64,512]{4,3,2,1,0:T(8,128)S(1)}, f32[1,4,8,64,512]{4,3,2,1,0:T(8,128)}, u32[]{:S(2)}) %copy-start.2) | copy-done | bytes 4194328
  25.1 0.6 shard_map.69.own_ref
  25.7 1.9 %collective-permute-done.2.a2_ref = bf16[8,64,256]{2,1,0:T(8,128)(2,1)S(1)} collective-permute-done((bf16[8,64,256]{2,1,0:T(8,128)(2,1)S(1)}, bf16[8,64,256]{2,1,0:T(8,128)(2,1)S(1)}, u32[]{:S(2)}, u32[]{:S(2)}) %collective-permute-start.2) | collective-permute-done | bytes 262176 | tf_op jit(solution)/shard_map/ppermute | solution.py:97
  27.6 1.2 %collective-permute-done.3.b2_ref = bf16[8,64,256]{2,1,0:T(8,128)(2,1)S(1)} collective-permute-done((bf16[8,64,256]{2,1,0:T(8,128)(2,1)S(1)}, bf16[8,64,256]{2,1,0:T(8,128)(2,1)S(1)}, u32[]{:S(2)}, u32[]{:S(2)}) %collective-permute-start.3) | collective-permute-done | bytes 262176 | tf_op jit(solution)/shard_map/ppermute | solution.py:97
  29.5 1.5 %collective-permute-done.4.other_ref = bf16[8,64,512]{2,1,0:T(8,128)(2,1)S(1)} collective-permute-done((bf16[8,64,512]{2,1,0:T(8,128)(2,1)S(1)}, bf16[8,64,512]{2,1,0:T(8,128)(2,1)S(1)}, u32[]{:S(2)}, u32[]{:S(2)}) %collective-permute-start.4) | collective-permute-done | bytes 524320 | tf_op jit(solution)/shard_map/ppermute | solution.py:333
  30.9 0.6 shard_map.73
  31.6 1.6 %collective-permute-start.5 = (bf16[2,64,512]{2,1,0:T(8,128)(2,1)S(1)}, bf16[2,64,512]{2,1,0:T(8,128)(2,1)S(1)}, u32[]{:S(2)}, u32[]{:S(2)}) collective-permute-start(bf16[2,64,512]{2,1,0:T(8,128)(2,1)S(1)} %get-tuple-element.44), channel_id=1, source_target_pairs={{0,2},{1,3},{2,0},{3,1},{4,6},{5,7},{6,4},{7,5},{8,10},{9,11},{10,... | collective-permute-start | bytes 393224 | tf_op jit(solution)/shard_map/ppermute | solution.py:151
  33.2 2.6 %collective-permute-start.6 = (bf16[2,64,512]{2,1,0:T(8,128)(2,1)S(1)}, bf16[2,64,512]{2,1,0:T(8,128)(2,1)S(1)}, u32[]{:S(2)}, u32[]{:S(2)}) collective-permute-start(bf16[2,64,512]{2,1,0:T(8,128)(2,1)S(1)} %get-tuple-element.45), channel_id=1, source_target_pairs={{0,4},{1,5},{2,6},{3,7},{4,0},{5,1},{6,2},{7,3},{8,12},{9,13},{10,... | collective-permute-start | bytes 393224 | tf_op jit(solution)/shard_map/ppermute | solution.py:151
  36.0 1.6 %copy-done.4 = f32[1,1,2,512,512]{4,3,2,1,0:T(8,128)S(1)} copy-done((f32[1,1,2,512,512]{4,3,2,1,0:T(8,128)S(1)}, f32[1,1,2,512,512]{4,3,2,1,0:T(8,128)}, u32[]{:S(2)}) %copy-start.4) | copy-done | bytes 2097176
  37.9 1.2 %collective-permute-done.5.refs_1_ = bf16[2,64,512]{2,1,0:T(8,128)(2,1)S(1)} collective-permute-done((bf16[2,64,512]{2,1,0:T(8,128)(2,1)S(1)}, bf16[2,64,512]{2,1,0:T(8,128)(2,1)S(1)}, u32[]{:S(2)}, u32[]{:S(2)}) %collective-permute-start.5) | collective-permute-done | bytes 131104 | tf_op jit(solution)/shard_map/ppermute | solution.py:151
  39.1 7.0 %collective-permute-done.6.refs_2_ = bf16[2,64,512]{2,1,0:T(8,128)(2,1)S(1)} collective-permute-done((bf16[2,64,512]{2,1,0:T(8,128)(2,1)S(1)}, bf16[2,64,512]{2,1,0:T(8,128)(2,1)S(1)}, u32[]{:S(2)}, u32[]{:S(2)}) %collective-permute-start.6) | collective-permute-done | bytes 131104 | tf_op jit(solution)/shard_map/ppermute | solution.py:151
  46.1 9.0 %shard_map.74 = (bf16[2,64,512]{2,1,0:T(8,128)(2,1)S(1)}, bf16[2,64,512]{2,1,0:T(8,128)(2,1)S(1)}, bf16[2,64,512]{2,1,0:T(8,128)(2,1)S(1)}, bf16[2,64,512]{2,1,0...) custom-call(s32[35]{0:T(128)S(1)} %concatenate.4.scal, f32[2,512,512]{2,1,0:T(8,128)S(1)} %get-tuple-element.35.l_ref, ...), custom_call_target="tpu_custom_call" | custom-call | flops 5368709120 | bytes 4718732 | tf_op jit(solution)/shard_map/pallas_call | solution.py:34
  55.3 4.3 %collective-permute-start.10 = (bf16[2,64,512]{2,1,0:T(8,128)(2,1)S(1)}, bf16[2,64,512]{2,1,0:T(8,128)(2,1)S(1)}, u32[]{:S(2)}, u32[]{:S(2)}) collective-permute-start(bf16[2,64,512]{2,1,0:T(8,128)(2,1)S(1)} %get-tuple-element.50), channel_id=1, source_target_pairs={{0,6},{1,7},{2,4},{3,5},{4,2},{5,3},{6,0},{7,1},{8,14},{9,15},{10,... | collective-permute-start | bytes 393224 | tf_op jit(solution)/shard_map/ppermute | solution.py:151
  60.3 3.7 %collective-permute-start.14 = (bf16[2,64,512]{2,1,0:T(8,128)(2,1)S(1)}, bf16[2,64,512]{2,1,0:T(8,128)(2,1)S(1)}, u32[]{:S(2)}, u32[]{:S(2)}) collective-permute-start(bf16[2,64,512]{2,1,0:T(8,128)(2,1)S(1)} %get-tuple-element.54), channel_id=1, source_target_pairs={{0,6},{1,7},{2,4},{3,5},{4,2},{5,3},{6,0},{7,1},{8,14},{9,15},{10,... | collective-permute-start | bytes 393224 | tf_op jit(solution)/shard_map/ppermute | solution.py:151
  64.0 5.5 %collective-permute-done.9.refs_2_ = bf16[2,64,512]{2,1,0:T(8,128)(2,1)S(1)} collective-permute-done((bf16[2,64,512]{2,1,0:T(8,128)(2,1)S(1)}, bf16[2,64,512]{2,1,0:T(8,128)(2,1)S(1)}, u32[]{:S(2)}, u32[]{:S(2)}) %collective-permute-start.9) | collective-permute-done | bytes 131104 | tf_op jit(solution)/shard_map/ppermute | solution.py:151
  70.3 9.0 %collective-permute-done.13.refs_2_ = bf16[2,64,512]{2,1,0:T(8,128)(2,1)S(1)} collective-permute-done((bf16[2,64,512]{2,1,0:T(8,128)(2,1)S(1)}, bf16[2,64,512]{2,1,0:T(8,128)(2,1)S(1)}, u32[]{:S(2)}, u32[]{:S(2)}) %collective-permute-start.13) | collective-permute-done | bytes 131104 | tf_op jit(solution)/shard_map/ppermute | solution.py:151
  79.3 9.2 %shard_map.76 = (bf16[64,512]{1,0:T(8,128)(2,1)S(1)}, bf16[64,512]{1,0:T(8,128)(2,1)S(1)}, bf16[64,512]{1,0:T(8,128)(2,1)S(1)}, bf16[64,512]{1,0:T(8,128)(2,1)S(...) custom-call(s32[35]{0:T(128)S(1)} %concatenate.4.scal, ...), custom_call_target="tpu_custom_call", output_to_operand_aliasing={{8}: (7, {}), {9}: (8, {})} | custom-call | flops 5368709120 | bytes 8913036 | tf_op jit(solution)/shard_map/pallas_call | solution.py:34
  88.7 3.3 %collective-permute-start.16 = (bf16[64,512]{1,0:T(8,128)(2,1)S(1)}, bf16[64,512]{1,0:T(8,128)(2,1)S(1)}, u32[]{:S(2)}, u32[]{:S(2)}) collective-permute-start(bf16[64,512]{1,0:T(8,128)(2,1)S(1)} %get-tuple-element.59), channel_id=1, source_target_pairs={{0,2},{1,3},{2,0},{3,1},{4,6},{5,7},{6,4},{7,5},{8,10},{9,11},{10,... | collective-permute-start | bytes 196616 | tf_op jit(solution)/shard_map/ppermute | solution.py:151
  92.1 2.4 %collective-permute-start.19 = (bf16[64,512]{1,0:T(8,128)(2,1)S(1)}, bf16[64,512]{1,0:T(8,128)(2,1)S(1)}, u32[]{:S(2)}, u32[]{:S(2)}) collective-permute-start(bf16[64,512]{1,0:T(8,128)(2,1)S(1)} %get-tuple-element.62), channel_id=1, source_target_pairs={{0,5},{1,4},{2,7},{3,6},{4,1},{5,0},{6,3},{7,2},{8,13},{9,12},{10,... | collective-permute-start | bytes 196616 | tf_op jit(solution)/shard_map/ppermute | solution.py:151
  94.5 1.6 %collective-permute-start.20 = (bf16[64,512]{1,0:T(8,128)(2,1)S(1)}, bf16[64,512]{1,0:T(8,128)(2,1)S(1)}, u32[]{:S(2)}, u32[]{:S(2)}) collective-permute-start(bf16[64,512]{1,0:T(8,128)(2,1)S(1)} %get-tuple-element.63), channel_id=1, source_target_pairs={{0,6},{1,7},{2,4},{3,5},{4,2},{5,3},{6,0},{7,1},{8,14},{9,15},{10,... | collective-permute-start | bytes 196616 | tf_op jit(solution)/shard_map/ppermute | solution.py:151
  96.2 1.8 %collective-permute-done.17.refs_8_ = bf16[64,512]{1,0:T(8,128)(2,1)S(1)} collective-permute-done((bf16[64,512]{1,0:T(8,128)(2,1)S(1)}, bf16[64,512]{1,0:T(8,128)(2,1)S(1)}, u32[]{:S(2)}, u32[]{:S(2)}) %collective-permute-start.17) | collective-permute-done | bytes 65568 | tf_op jit(solution)/shard_map/ppermute | solution.py:151
  98.3 3.9 %collective-permute-done.18.refs_9_ = bf16[64,512]{1,0:T(8,128)(2,1)S(1)} collective-permute-done((bf16[64,512]{1,0:T(8,128)(2,1)S(1)}, bf16[64,512]{1,0:T(8,128)(2,1)S(1)}, u32[]{:S(2)}, u32[]{:S(2)}) %collective-permute-start.18) | collective-permute-done | bytes 65568 | tf_op jit(solution)/shard_map/ppermute | solution.py:151
  102.2 1.8 %collective-permute-done.21.refs_12_ = bf16[64,512]{1,0:T(8,128)(2,1)S(1)} collective-permute-done((bf16[64,512]{1,0:T(8,128)(2,1)S(1)}, bf16[64,512]{1,0:T(8,128)(2,1)S(1)}, u32[]{:S(2)}, u32[]{:S(2)}) %collective-permute-start.21) | collective-permute-done | bytes 65568 | tf_op jit(solution)/shard_map/ppermute | solution.py:151
  104.0 1.5 %shard_map.77 = bf16[8,64,512]{2,1,0:T(8,128)(2,1)} custom-call(s32[35]{0:T(128)S(1)} %concatenate.4.scal, bf16[2,64,512]{2,1,0:T(8,128)(2,1)S(1)} %get-tuple-element.47.refs_0_, bf16[2,64,512]{2,1,0:T(8,128)(2,1)S(1)} %collective-permute-done.8.refs_1_, bf16[2,64,512]{2,1,0:T(8,128)(2,1)S(1)} %collective-permute-done.9.refs_2_, ...), custom_call_target="tpu_custom_call" | custom-call | bytes 1310860 | tf_op jit(solution)/shard_map/pallas_call | solution.py:34
  (42 shorter events, 4.6 us)
Async XLA Ops:
  0.6 22.2 %copy-start = (s32[4,8]{1,0:T(4,128)S(1)}, s32[4,8]{1,0:T(4,128)}, u32[]{:S(2)}) copy-start(s32[4,8]{1,0:T(4,128)} %param.5) | copy-start | bytes 388
  0.7 2.2 %copy-start.1 = (f32[1,4,8,64,512]{4,3,2,1,0:T(8,128)S(1)}, f32[1,4,8,64,512]{4,3,2,1,0:T(8,128)}, u32[]{:S(2)}) copy-start(f32[1,4,8,64,512]{4,3,2,1,0:T(8,128)} %param.4) | copy-start | bytes 12582916
  3.6 15.0 %collective-permute-start = (bf16[2,8,64,256]{3,2,1,0:T(8,128)(2,1)S(1)}, bf16[2,8,64,256]{3,2,1,0:T(8,128)(2,1)S(1)}, u32[]{:S(2)}, u32[]{:S(2)}) collective-permute-start(bf16[2,8,64,256]{3,2,1,0:T(8,128)(2,1)S(1)} %get-tuple-element.37), channel_id=1, source_target_pairs={{0,8},{8,0},{16,24},{24,16},{1,9},{9,1},{17,25},{25,17},{2,10},{10... | collective-permute-start | bytes 1572872 | tf_op jit(solution)/shard_map/ppermute | solution.py:91
  6.6 13.4 %collective-permute-start.1 = (bf16[2,8,64,256]{3,2,1,0:T(8,128)(2,1)S(1)}, bf16[2,8,64,256]{3,2,1,0:T(8,128)(2,1)S(1)}, u32[]{:S(2)}, u32[]{:S(2)}) collective-permute-start(bf16[2,8,64,256]{3,2,1,0:T(8,128)(2,1)S(1)} %get-tuple-element.38), channel_id=1, source_target_pairs={{0,16},{8,24},{16,0},{24,8},{1,17},{9,25},{17,1},{25,9},{2,18},{10... | collective-permute-start | bytes 1572872 | tf_op jit(solution)/shard_map/ppermute | solution.py:91
  20.7 7.0 %collective-permute-start.2 = (bf16[8,64,256]{2,1,0:T(8,128)(2,1)S(1)}, bf16[8,64,256]{2,1,0:T(8,128)(2,1)S(1)}, u32[]{:S(2)}, u32[]{:S(2)}) collective-permute-start(bf16[8,64,256]{2,1,0:T(8,128)(2,1)S(1)} %get-tuple-element.41), channel_id=1, source_target_pairs={{0,16},{8,24},{16,0},{24,8},{1,17},{9,25},{17,1},{25,9},{2,18},{10... | collective-permute-start | bytes 786440 | tf_op jit(solution)/shard_map/ppermute | solution.py:97
  22.3 6.6 %collective-permute-start.3 = (bf16[8,64,256]{2,1,0:T(8,128)(2,1)S(1)}, bf16[8,64,256]{2,1,0:T(8,128)(2,1)S(1)}, u32[]{:S(2)}, u32[]{:S(2)}) collective-permute-start(bf16[8,64,256]{2,1,0:T(8,128)(2,1)S(1)} %get-tuple-element.42), channel_id=1, source_target_pairs={{0,8},{8,0},{16,24},{24,16},{1,9},{9,1},{17,25},{25,17},{2,10},{10... | collective-permute-start | bytes 786440 | tf_op jit(solution)/shard_map/ppermute | solution.py:97
  22.9 2.2 %copy-start.2 = (f32[1,4,8,64,512]{4,3,2,1,0:T(8,128)S(1)}, f32[1,4,8,64,512]{4,3,2,1,0:T(8,128)}, u32[]{:S(2)}) copy-start(f32[1,4,8,64,512]{4,3,2,1,0:T(8,128)} %param.4) | copy-start | bytes 12582916
  25.7 10.3 %copy-start.3 = (f32[1,1,2,512,512]{4,3,2,1,0:T(8,128)S(1)}, f32[1,1,2,512,512]{4,3,2,1,0:T(8,128)}, u32[]{:S(2)}) copy-start(f32[1,1,2,512,512]{4,3,2,1,0:T(8,128)} %param.6) | copy-start | bytes 6291460
  29.0 2.0 %collective-permute-start.4 = (bf16[8,64,512]{2,1,0:T(8,128)(2,1)S(1)}, bf16[8,64,512]{2,1,0:T(8,128)(2,1)S(1)}, u32[]{:S(2)}, u32[]{:S(2)}) collective-permute-start(bf16[8,64,512]{2,1,0:T(8,128)(2,1)S(1)} %shard_map.72.own_ref), channel_id=1, source_target_pairs={{0,1},{1,0},{2,3},{3,2},{4,5},{5,4},{6,7},{7,6},{8,9},{9,8},{10,11... | collective-permute-start | bytes 1572872 | tf_op jit(solution)/shard_map/ppermute | solution.py:333
  31.6 7.5 %collective-permute-start.5 = (bf16[2,64,512]{2,1,0:T(8,128)(2,1)S(1)}, bf16[2,64,512]{2,1,0:T(8,128)(2,1)S(1)}, u32[]{:S(2)}, u32[]{:S(2)}) collective-permute-start(bf16[2,64,512]{2,1,0:T(8,128)(2,1)S(1)} %get-tuple-element.44), channel_id=1, source_target_pairs={{0,2},{1,3},{2,0},{3,1},{4,6},{5,7},{6,4},{7,5},{8,10},{9,11},{10,... | collective-permute-start | bytes 393224 | tf_op jit(solution)/shard_map/ppermute | solution.py:151
  33.2 12.9 %collective-permute-start.6 = (bf16[2,64,512]{2,1,0:T(8,128)(2,1)S(1)}, bf16[2,64,512]{2,1,0:T(8,128)(2,1)S(1)}, u32[]{:S(2)}, u32[]{:S(2)}) collective-permute-start(bf16[2,64,512]{2,1,0:T(8,128)(2,1)S(1)} %get-tuple-element.45), channel_id=1, source_target_pairs={{0,4},{1,5},{2,6},{3,7},{4,0},{5,1},{6,2},{7,3},{8,12},{9,13},{10,... | collective-permute-start | bytes 393224 | tf_op jit(solution)/shard_map/ppermute | solution.py:151
  35.8 10.3 %collective-permute-start.7 = (bf16[2,64,512]{2,1,0:T(8,128)(2,1)S(1)}, bf16[2,64,512]{2,1,0:T(8,128)(2,1)S(1)}, u32[]{:S(2)}, u32[]{:S(2)}) collective-permute-start(bf16[2,64,512]{2,1,0:T(8,128)(2,1)S(1)} %get-tuple-element.46), channel_id=1, source_target_pairs={{0,6},{1,7},{2,4},{3,5},{4,2},{5,3},{6,0},{7,1},{8,14},{9,15},{10,... | collective-permute-start | bytes 393224 | tf_op jit(solution)/shard_map/ppermute | solution.py:151
  36.0 1.6 %copy-start.4 = (f32[1,1,2,512,512]{4,3,2,1,0:T(8,128)S(1)}, f32[1,1,2,512,512]{4,3,2,1,0:T(8,128)}, u32[]{:S(2)}) copy-start(f32[1,1,2,512,512]{4,3,2,1,0:T(8,128)} %param.7) | copy-start | bytes 6291460
  55.2 5.1 %collective-permute-start.8 = (bf16[2,64,512]{2,1,0:T(8,128)(2,1)S(1)}, bf16[2,64,512]{2,1,0:T(8,128)(2,1)S(1)}, u32[]{:S(2)}, u32[]{:S(2)}) collective-permute-start(bf16[2,64,512]{2,1,0:T(8,128)(2,1)S(1)} %get-tuple-element.48), channel_id=1, source_target_pairs={{0,2},{1,3},{2,0},{3,1},{4,6},{5,7},{6,4},{7,5},{8,10},{9,11},{10,... | collective-permute-start | bytes 393224 | tf_op jit(solution)/shard_map/ppermute | solution.py:151
  55.2 14.3 %collective-permute-start.9 = (bf16[2,64,512]{2,1,0:T(8,128)(2,1)S(1)}, bf16[2,64,512]{2,1,0:T(8,128)(2,1)S(1)}, u32[]{:S(2)}, u32[]{:S(2)}) collective-permute-start(bf16[2,64,512]{2,1,0:T(8,128)(2,1)S(1)} %get-tuple-element.49), channel_id=1, source_target_pairs={{0,4},{1,5},{2,6},{3,7},{4,0},{5,1},{6,2},{7,3},{8,12},{9,13},{10,... | collective-permute-start | bytes 393224 | tf_op jit(solution)/shard_map/ppermute | solution.py:151
  55.3 14.2 %collective-permute-start.10 = (bf16[2,64,512]{2,1,0:T(8,128)(2,1)S(1)}, bf16[2,64,512]{2,1,0:T(8,128)(2,1)S(1)}, u32[]{:S(2)}, u32[]{:S(2)}) collective-permute-start(bf16[2,64,512]{2,1,0:T(8,128)(2,1)S(1)} %get-tuple-element.50), channel_id=1, source_target_pairs={{0,6},{1,7},{2,4},{3,5},{4,2},{5,3},{6,0},{7,1},{8,14},{9,15},{10,... | collective-permute-start | bytes 393224 | tf_op jit(solution)/shard_map/ppermute | solution.py:151
  59.6 10.7 %collective-permute-start.12 = (bf16[2,64,512]{2,1,0:T(8,128)(2,1)S(1)}, bf16[2,64,512]{2,1,0:T(8,128)(2,1)S(1)}, u32[]{:S(2)}, u32[]{:S(2)}) collective-permute-start(bf16[2,64,512]{2,1,0:T(8,128)(2,1)S(1)} %get-tuple-element.52), channel_id=1, source_target_pairs={{0,2},{1,3},{2,0},{3,1},{4,6},{5,7},{6,4},{7,5},{8,10},{9,11},{10,... | collective-permute-start | bytes 393224 | tf_op jit(solution)/shard_map/ppermute | solution.py:151
  59.6 19.6 %collective-permute-start.13 = (bf16[2,64,512]{2,1,0:T(8,128)(2,1)S(1)}, bf16[2,64,512]{2,1,0:T(8,128)(2,1)S(1)}, u32[]{:S(2)}, u32[]{:S(2)}) collective-permute-start(bf16[2,64,512]{2,1,0:T(8,128)(2,1)S(1)} %get-tuple-element.53), channel_id=1, source_target_pairs={{0,4},{1,5},{2,6},{3,7},{4,0},{5,1},{6,2},{7,3},{8,12},{9,13},{10,... | collective-permute-start | bytes 393224 | tf_op jit(solution)/shard_map/ppermute | solution.py:151
  60.3 19.0 %collective-permute-start.14 = (bf16[2,64,512]{2,1,0:T(8,128)(2,1)S(1)}, bf16[2,64,512]{2,1,0:T(8,128)(2,1)S(1)}, u32[]{:S(2)}, u32[]{:S(2)}) collective-permute-start(bf16[2,64,512]{2,1,0:T(8,128)(2,1)S(1)} %get-tuple-element.54), channel_id=1, source_target_pairs={{0,6},{1,7},{2,4},{3,5},{4,2},{5,3},{6,0},{7,1},{8,14},{9,15},{10,... | collective-permute-start | bytes 393224 | tf_op jit(solution)/shard_map/ppermute | solution.py:151
  70.1 33.9 %collective-permute-start.11 = (bf16[4,64,512]{2,1,0:T(8,128)(2,1)S(1)}, bf16[4,64,512]{2,1,0:T(8,128)(2,1)S(1)}, u32[]{:S(2)}, u32[]{:S(2)}) collective-permute-start(bf16[4,64,512]{2,1,0:T(8,128)(2,1)S(1)} %shard_map.75), channel_id=1, source_target_pairs={{0,1},{1,0},{2,3},{3,2},{4,5},{5,4},{6,7},{7,6},{8,9},{9,8},{10,11... | collective-permute-start | bytes 786440 | tf_op jit(solution)/shard_map/ppermute | solution.py:359
  88.5 3.5 %collective-permute-start.15 = (bf16[64,512]{1,0:T(8,128)(2,1)S(1)}, bf16[64,512]{1,0:T(8,128)(2,1)S(1)}, u32[]{:S(2)}, u32[]{:S(2)}) collective-permute-start(bf16[64,512]{1,0:T(8,128)(2,1)S(1)} %get-tuple-element.58), channel_id=1, source_target_pairs={{0,1},{1,0},{2,3},{3,2},{4,5},{5,4},{6,7},{7,6},{8,9},{9,8},{10,11... | collective-permute-start | bytes 196616 | tf_op jit(solution)/shard_map/ppermute | solution.py:151
  88.7 5.8 %collective-permute-start.16 = (bf16[64,512]{1,0:T(8,128)(2,1)S(1)}, bf16[64,512]{1,0:T(8,128)(2,1)S(1)}, u32[]{:S(2)}, u32[]{:S(2)}) collective-permute-start(bf16[64,512]{1,0:T(8,128)(2,1)S(1)} %get-tuple-element.59), channel_id=1, source_target_pairs={{0,2},{1,3},{2,0},{3,1},{4,6},{5,7},{6,4},{7,5},{8,10},{9,11},{10,... | collective-permute-start | bytes 196616 | tf_op jit(solution)/shard_map/ppermute | solution.py:151
  92.0 5.9 %collective-permute-start.17 = (bf16[64,512]{1,0:T(8,128)(2,1)S(1)}, bf16[64,512]{1,0:T(8,128)(2,1)S(1)}, u32[]{:S(2)}, u32[]{:S(2)}) collective-permute-start(bf16[64,512]{1,0:T(8,128)(2,1)S(1)} %get-tuple-element.60), channel_id=1, source_target_pairs={{0,3},{1,2},{2,1},{3,0},{4,7},{5,6},{6,5},{7,4},{8,11},{9,10},{10,... | collective-permute-start | bytes 196616 | tf_op jit(solution)/shard_map/ppermute | solution.py:151
  92.0 10.1 %collective-permute-start.18 = (bf16[64,512]{1,0:T(8,128)(2,1)S(1)}, bf16[64,512]{1,0:T(8,128)(2,1)S(1)}, u32[]{:S(2)}, u32[]{:S(2)}) collective-permute-start(bf16[64,512]{1,0:T(8,128)(2,1)S(1)} %get-tuple-element.61), channel_id=1, source_target_pairs={{0,4},{1,5},{2,6},{3,7},{4,0},{5,1},{6,2},{7,3},{8,12},{9,13},{10,... | collective-permute-start | bytes 196616 | tf_op jit(solution)/shard_map/ppermute | solution.py:151
  92.1 10.1 %collective-permute-start.19 = (bf16[64,512]{1,0:T(8,128)(2,1)S(1)}, bf16[64,512]{1,0:T(8,128)(2,1)S(1)}, u32[]{:S(2)}, u32[]{:S(2)}) collective-permute-start(bf16[64,512]{1,0:T(8,128)(2,1)S(1)} %get-tuple-element.62), channel_id=1, source_target_pairs={{0,5},{1,4},{2,7},{3,6},{4,1},{5,0},{6,3},{7,2},{8,13},{9,12},{10,... | collective-permute-start | bytes 196616 | tf_op jit(solution)/shard_map/ppermute | solution.py:151
  94.5 7.6 %collective-permute-start.20 = (bf16[64,512]{1,0:T(8,128)(2,1)S(1)}, bf16[64,512]{1,0:T(8,128)(2,1)S(1)}, u32[]{:S(2)}, u32[]{:S(2)}) collective-permute-start(bf16[64,512]{1,0:T(8,128)(2,1)S(1)} %get-tuple-element.63), channel_id=1, source_target_pairs={{0,6},{1,7},{2,4},{3,5},{4,2},{5,3},{6,0},{7,1},{8,14},{9,15},{10,... | collective-permute-start | bytes 196616 | tf_op jit(solution)/shard_map/ppermute | solution.py:151
  97.9 6.0 %collective-permute-start.21 = (bf16[64,512]{1,0:T(8,128)(2,1)S(1)}, bf16[64,512]{1,0:T(8,128)(2,1)S(1)}, u32[]{:S(2)}, u32[]{:S(2)}) collective-permute-start(bf16[64,512]{1,0:T(8,128)(2,1)S(1)} %get-tuple-element.64), channel_id=1, source_target_pairs={{0,7},{1,6},{2,5},{3,4},{4,3},{5,2},{6,1},{7,0},{8,15},{9,14},{10,... | collective-permute-start | bytes 196616 | tf_op jit(solution)/shard_map/ppermute | solution.py:151

commit v2 on v1

--- a/solution.py
+++ b/solution.py
@@ -10,6 +10,7 @@
 
 MOST = 2
 POWER = 8
+CENTER = 3.6
 
 decay_rate = 0.9
 damping = 0.1
@@ -65,10 +66,8 @@
     own_ref[:, :, cut:] = p_ref[high, low, :, :, cut:] + b1_ref[low].astype(f32)
 
 
-def forward_kernel(scal, pa_ref, pb_ref, a1_ref, b1_ref, a_ref, b_ref):
-    high, low = scal[0], scal[1]
-    a_ref[...] = (pa_ref[...] + a1_ref[1 - high].astype(f32)).astype(bf16)
-    b_ref[...] = (pb_ref[...] + b1_ref[1 - low].astype(f32)).astype(bf16)
+def forward_kernel(bit, scal, kept_ref, first_ref, out_ref):
+    out_ref[...] = (kept_ref[...] + first_ref[1 - scal[bit]].astype(f32)).astype(bf16)
 
 
 def total_kernel(own_ref, a2_ref, b2_ref, out_ref):
@@ -92,9 +91,11 @@
     kept = [(jax.ShapeDtypeStruct(shape, f32), VMEM)] * 2
     pa, pb = call(keep_kernel, kept, [], fixed)
     arrived = [(array, VMEM) for array in first]
-    operands = [(scal, SMEM), (pa, VMEM), (pb, VMEM)] + arrived
-    a, b = call(forward_kernel, [one] * 2, [], operands)
-    second = [lax.ppermute(a, "dp", over_high), lax.ppermute(b, "dp", over_low)]
+    second = []
+    for bit, (kept, perm) in enumerate([(pa, over_high), (pb, over_low)]):
+        operands = [(scal, SMEM), (kept, VMEM), (first[bit], VMEM)]
+        (summed,) = call(functools.partial(forward_kernel, bit), [one], [], operands)
+        second.append(lax.ppermute(summed, "dp", perm))
     whole = [(jax.ShapeDtypeStruct((count, stripe, size), f32), VMEM)]
     (own,) = call(half_kernel, whole, [], fixed + arrived)
     operands = [(own, VMEM)] + [(array, VMEM) for array in second]
@@ -147,11 +148,11 @@
 
 
 def over_block(arrays, count, stride):
-    return [arrays[0]] + [
-        lax.ppermute(array, "block", [(i, i ^ (r * stride)) for i in range(count)])
-        for r, array in enumerate(arrays)
-        if r > 0
-    ]
+    moved = [arrays[0]]
+    for r in range(1, len(arrays)):
+        pairs = [(i, i ^ (r * stride)) for i in range(count)]
+        moved.append(lax.ppermute(arrays[r], "block", pairs))
+    return moved
 
 
 def add_diagonal(ref, k, value):
@@ -165,13 +166,55 @@
         ref[k, part, part] += spread
 
 
+def times_row(ref, k, row):
+    size = ref.shape[1]
+    step = min(size, 64)
+    return jnp.concatenate(
+        [
+            jnp.sum(ref[k, pl.ds(start, step), :] * row, axis=1, keepdims=True)
+            for start in range(0, size, step)
+        ]
+    )
+
+
+def times_column(ref, k, column):
+    total = 0.0
+    for start in range(0, ref.shape[1], 8):
+        total += ref[k, pl.ds(start, 8), :] * column[start : start + 8]
+    return jnp.sum(total, axis=0, keepdims=True)
+
+
+def product(a_ref, b_ref, k):
+    half = a_ref.shape[1] // 2
+    return mm(a_ref[k, :half, :], b_ref[k]), mm(a_ref[k, half:, :], b_ref[k, :, half:])
+
+
+def upper(ref, k):
+    half = ref.shape[1] // 2
+    return ref[k, :half, :], ref[k, half:, half:]
+
+
+def store(ref, k, blocks):
+    half = ref.shape[1] // 2
+    ref[k, :half, :] = blocks[0]
+    ref[k, half:, half:] = blocks[1]
+
+
+def mirror(ref, k, blocks):
+    half = ref.shape[1] // 2
+    top = blocks[0].astype(bf16)
+    ref[k, :half, :] = top
+    ref[k, half:, half:] = blocks[1].astype(bf16)
+    ref[k, half:, :half] = top[:, half:].T
+
+
 def slot_kernel(slot, direct, count, scal, l_ref, r_ref, *refs):
     chips = count // 2
     in_refs, refs = refs[:chips], refs[chips + (2 if slot else 0) :]
     n_out = count if direct else chips
     out_refs, refs = refs[:n_out], refs[n_out:]
-    lo_hbm, ro_hbm, g_ref, n_ref, *wides, y_ref = refs[:7]
-    mb_narrow, tb_narrow, ub_ref, yb_ref, out_sem = refs[7:]
+    lo_hbm, ro_hbm, g_ref, n_ref, m_ref, t_ref, y_ref, w_ref = refs[:8]
+    mb_ref, tb_ref, ub_ref, vb_ref, out_sem = refs[8:]
     size = g_ref.shape[0]
     stripe = size // count
     me = scal[2]
@@ -184,8 +227,6 @@
 
     @pl.when(active)
     def _():
-        m_ref, t_ref = wides
-        mb_ref, tb_ref = mb_narrow, tb_narrow
         for r, ref in enumerate(in_refs):
             for c in range(2):
                 start = pl.multiple_of((lax.bitwise_xor(chip, r) * 2 + c) * stripe, stripe)
@@ -206,7 +247,7 @@
         lengths = [None, None]
         for turn in range(POWER):
             for k in sides:
-                vectors[k] = jnp.sum(m_ref[k] * vectors[k], axis=1 - turn % 2, keepdims=True)
+                vectors[k] = (times_column if turn % 2 else times_row)(m_ref, k, vectors[k])
             for k in sides:
                 square = jnp.sum(vectors[k] * vectors[k], axis=turn % 2, keepdims=True)
                 lengths[k] = jnp.sqrt(square)
@@ -219,32 +260,47 @@
             scaled = m_ref[k] * (1.0 / ceiling)
             m_ref[k] = scaled
             mb_ref[k] = scaled.astype(bf16)
-        for step in range(2):
-            for k in sides:
-                t = mm(mb_ref[k], mb_ref[k]) * (1 / 16) - 0.625 * m_ref[k]
-                t_ref[k] = t
-                tb_ref[k] = t.astype(bf16)
-            for k in sides:
-                ub_ref[k] = (3.125 * t_ref[k] + mm(tb_ref[k], tb_ref[k])).astype(bf16)
-            for k in sides:
-                t = (625 / 256) * m_ref[k] + mm(ub_ref[k], mb_ref[k])
-                t_ref[k] = t
-                tb_ref[k] = t.astype(bf16)
-            if step == 0:
-                for k in sides:
-                    y = mm(mb_ref[k], tb_ref[k]) * (1 / 16) - 0.3125 * (m_ref[k] + t_ref[k])
-                    y_ref[k] = y
-                    yb_ref[k] = y.astype(bf16)
-                m_ref, t_ref = t_ref, m_ref
-                mb_ref, tb_ref = tb_ref, mb_ref
-        for k in sides:
-            x = 1.25 * y_ref[k] - (25 / 64) * t_ref[k] - 0.25 * mm(yb_ref[k], tb_ref[k])
-            m_ref[k] = x * scales[k]
+        for k in sides:
+            t = [p * (1 / 16) - 0.625 * m for p, m in zip(product(mb_ref, mb_ref, k), upper(m_ref, k))]
+            store(t_ref, k, t)
+            mirror(tb_ref, k, t)
+            mirror(vb_ref, k, [4.0 * x + 1.25 * m for x, m in zip(t, upper(m_ref, k))])
+        for k in sides:
+            mirror(ub_ref, k, [3.125 * t + p for t, p in zip(upper(t_ref, k), product(tb_ref, tb_ref, k))])
+        for k in sides:
+            y = [
+                0.25 * p + (625 / 256) * t + (1.25 * 625 / 1024 - 0.3125) * m
+                for p, t, m in zip(product(ub_ref, vb_ref, k), upper(t_ref, k), upper(m_ref, k))
+            ]
+            store(y_ref, k, y)
+            mirror(tb_ref, k, y)
+        for k in sides:
+            t = [3.125 * y + p for y, p in zip(upper(y_ref, k), product(tb_ref, tb_ref, k))]
+            store(t_ref, k, t)
+            mirror(vb_ref, k, t)
+        for k in sides:
+            store(
+                w_ref,
+                k,
+                [(625 / 128) * t + p for t, p in zip(upper(t_ref, k), product(vb_ref, vb_ref, k))],
+            )
+            add_diagonal(w_ref, k, jnp.full((1, 1), (625 / 256) ** 2 - CENTER, f32))
+            mirror(ub_ref, k, upper(w_ref, k))
+        for k in sides:
+            t = [CENTER * m + p for m, p in zip(upper(m_ref, k), product(ub_ref, mb_ref, k))]
+            store(t_ref, k, t)
+            mirror(vb_ref, k, t)
+        for k in sides:
+            x = [
+                (1.25 * y - (25 / 64) * t - 0.25 * p) * scales[k]
+                for y, t, p in zip(upper(y_ref, k), upper(t_ref, k), product(tb_ref, vb_ref, k))
+            ]
+            store(m_ref, k, x)
             add_diagonal(m_ref, k, (125 / 64) * scales[k])
-            mb_ref[k] = m_ref[k].astype(bf16)
-
-        mb_ref[0] = mm(mb_ref[0], g).astype(bf16)
-        shaped = mm(mb_ref[0], mb_ref[1])
+            mirror(mb_ref, k, upper(m_ref, k))
+
+        tb_ref[0] = mm(mb_ref[0], g).astype(bf16)
+        shaped = mm(tb_ref[0], mb_ref[1])
         m_ref[0] = shaped
         wide = g.astype(f32)
         entries = size * size
@@ -294,7 +350,7 @@
     *updates, new_left, new_right = call(
         functools.partial(slot_kernel, slot, direct, count),
         out + news,
-        [pltpu.VMEM((size, size), bf16)] + [wide] * 4 + [narrow] * 4 + [sem],
+        [pltpu.VMEM((size, size), bf16)] + [wide] * 5 + [narrow] * 4 + [sem],
         operands,
         flops=40 * size**3,
         aliases=aliases,
@@ -340,7 +396,8 @@
     )
     pieces = []
     for slot in range(MOST):
-        pieces.append(over_block(messages[slot * chips : (slot + 1) * chips], count, 2))
+        part = messages[slot * chips : (slot + 1) * chips]
+        pieces.append(over_block(part, count, 2))
 
     states = [(state, VMEM) for state in (left, right)]
     kept = [(jax.ShapeDtypeStruct(left.shape, f32), VMEM)] * 2

time: 106 us -> 103 us (0.972)
  waiting for transfers between devices: 46.3 us -> 44.1 us
  Pallas kernels: 23.9 us -> 22 us
  starting transfers between devices: 27.9 us -> 29.2 us
    pallas_call x11 -> x12, Pallas kernels: 23.9 us -> 22 us  [call(): pl.pallas_call(kernel, in_specs=[pl.BlockSpec(memory_space=space) for _,...]
    ppermute x2, waiting for transfers between devices: 11.2 us -> 9.78 us  [sum_over_dp(): first = [lax.ppermute(a, 'dp', over_low), lax.ppermute(b, 'dp', over_high)]]
    ppermute x18, starting transfers between devices: 23.1 us -> 24.4 us  [the longest x16 21 us: over_block(): moved.append(lax.ppermute(arrays[r], 'block', pairs))]
  transfers between devices with their start and end apart: 22 -> 22, of which waited for: 14 -> 13; matrix products, arithmetic and copies ran while one was open for 0% -> 0% of each run, Pallas kernels for 11% -> 11%
where the time goes in v2:
time: 103 us
  waiting for transfers between devices  44.1 us (43%)
  starting transfers between devices  29.2 us (28%)
  Pallas kernels  22 us (21%)
  local copies, waits for them, and re-layouts  6.23 us (6%)
    ppermute x16, waiting for transfers between devices, over_block(): moved.append(lax.ppermute(arrays[r], 'block', pairs))  30.4 us
    pallas_call x12, Pallas kernels, call(): pl.pallas_call(kernel, in_specs=[pl.BlockSpec(memory_space=space) for _,...  22 us
    ppermute x16, starting transfers between devices, over_block(): moved.append(lax.ppermute(arrays[r], 'block', pairs))  21 us
    ppermute x2, waiting for transfers between devices, sum_over_dp(): first = [lax.ppermute(a, 'dp', over_low), lax.ppermute(b, 'dp', over_high)]  9.78 us
    unnamed x10, local copies, waits for them, and re-layouts  5.98 us
    ppermute x2, starting transfers between devices, sum_over_dp(): first = [lax.ppermute(a, 'dp', over_low), lax.ppermute(b, 'dp', over_high)]  4.55 us
    ppermute x2, starting transfers between devices, sum_over_dp(): second.append(lax.ppermute(summed, 'dp', perm))  3.39 us
    ppermute x2, waiting for transfers between devices, sum_over_dp(): second.append(lax.ppermute(summed, 'dp', perm))  2.48 us
  transfers between devices with their start and end apart: 22, of which 13 were waited for; matrix products, arithmetic and copies ran while one was open for 0% of the time, Pallas kernels for 11%

profile of v2, /device:TPU:0, one launch (start us, length us, event | category | flops | bytes accessed | tf_op | source)
XLA Modules:
  0.0 102.7 jit_solution(15552378384674657435)
XLA Ops:
  0.7 2.2 %copy-done.1 = f32[1,4,8,64,512]{4,3,2,1,0:T(8,128)S(1)} copy-done((f32[1,4,8,64,512]{4,3,2,1,0:T(8,128)S(1)}, f32[1,4,8,64,512]{4,3,2,1,0:T(8,128)}, u32[]{:S(2)}) %copy-start.1) | copy-done | bytes 4194328
  2.9 0.7 shard_map.68
  3.6 3.0 %collective-permute-start = (bf16[2,8,64,256]{3,2,1,0:T(8,128)(2,1)S(1)}, bf16[2,8,64,256]{3,2,1,0:T(8,128)(2,1)S(1)}, u32[]{:S(2)}, u32[]{:S(2)}) collective-permute-start(bf16[2,8,64,256]{3,2,1,0:T(8,128)(2,1)S(1)} %get-tuple-element.35), channel_id=1, source_target_pairs={{0,8},{8,0},{16,24},{24,16},{1,9},{9,1},{17,25},{25,17},{2,10},{10... | collective-permute-start | bytes 1572872 | tf_op jit(solution)/shard_map/ppermute | solution.py:90
  6.6 1.5 %collective-permute-start.1 = (bf16[2,8,64,256]{3,2,1,0:T(8,128)(2,1)S(1)}, bf16[2,8,64,256]{3,2,1,0:T(8,128)(2,1)S(1)}, u32[]{:S(2)}, u32[]{:S(2)}) collective-permute-start(bf16[2,8,64,256]{3,2,1,0:T(8,128)(2,1)S(1)} %get-tuple-element.36), channel_id=1, source_target_pairs={{0,16},{8,24},{16,0},{24,8},{1,17},{9,25},{17,1},{25,9},{2,18},{10... | collective-permute-start | bytes 1572872 | tf_op jit(solution)/shard_map/ppermute | solution.py:90
  8.2 0.6 shard_map.70
  8.8 9.8 %collective-permute-done.a1_ref.first_ref = bf16[2,8,64,256]{3,2,1,0:T(8,128)(2,1)S(1)} collective-permute-done((bf16[2,8,64,256]{3,2,1,0:T(8,128)(2,1)S(1)}, bf16[2,8,64,256]{3,2,1,0:T(8,128)(2,1)S(1)}, u32[]{:S(2)}, u32[]{:S(2)}) %collective-permute-start) | collective-permute-done | bytes 524320 | tf_op jit(solution)/shard_map/ppermute | solution.py:90
  19.2 1.8 %collective-permute-start.2 = (bf16[8,64,256]{2,1,0:T(8,128)(2,1)S(1)}, bf16[8,64,256]{2,1,0:T(8,128)(2,1)S(1)}, u32[]{:S(2)}, u32[]{:S(2)}) collective-permute-start(bf16[8,64,256]{2,1,0:T(8,128)(2,1)S(1)} %shard_map.71), channel_id=1, source_target_pairs={{0,16},{8,24},{16,0},{24,8},{1,17},{9,25},{17,1},{25,9},{2,18},{10... | collective-permute-start | bytes 786440 | tf_op jit(solution)/shard_map/ppermute | solution.py:98
  21.6 1.6 %collective-permute-start.3 = (bf16[8,64,256]{2,1,0:T(8,128)(2,1)S(1)}, bf16[8,64,256]{2,1,0:T(8,128)(2,1)S(1)}, u32[]{:S(2)}, u32[]{:S(2)}) collective-permute-start(bf16[8,64,256]{2,1,0:T(8,128)(2,1)S(1)} %shard_map.72), channel_id=1, source_target_pairs={{0,8},{8,0},{16,24},{24,16},{1,9},{9,1},{17,25},{25,17},{2,10},{10... | collective-permute-start | bytes 786440 | tf_op jit(solution)/shard_map/ppermute | solution.py:98
  23.3 2.2 %copy-done.2 = f32[1,4,8,64,512]{4,3,2,1,0:T(8,128)S(1)} copy-done((f32[1,4,8,64,512]{4,3,2,1,0:T(8,128)S(1)}, f32[1,4,8,64,512]{4,3,2,1,0:T(8,128)}, u32[]{:S(2)}) %copy-start.2) | copy-done | bytes 4194328
  25.4 0.6 shard_map.69.own_ref
  26.1 0.6 collective-permute-done.2.a2_ref
  26.7 1.9 %collective-permute-done.3.b2_ref = bf16[8,64,256]{2,1,0:T(8,128)(2,1)S(1)} collective-permute-done((bf16[8,64,256]{2,1,0:T(8,128)(2,1)S(1)}, bf16[8,64,256]{2,1,0:T(8,128)(2,1)S(1)}, u32[]{:S(2)}, u32[]{:S(2)}) %collective-permute-start.3) | collective-permute-done | bytes 262176 | tf_op jit(solution)/shard_map/ppermute | solution.py:98
  29.2 1.5 %collective-permute-done.4.other_ref = bf16[8,64,512]{2,1,0:T(8,128)(2,1)S(1)} collective-permute-done((bf16[8,64,512]{2,1,0:T(8,128)(2,1)S(1)}, bf16[8,64,512]{2,1,0:T(8,128)(2,1)S(1)}, u32[]{:S(2)}, u32[]{:S(2)}) %collective-permute-start.4) | collective-permute-done | bytes 524320 | tf_op jit(solution)/shard_map/ppermute | solution.py:389
  30.6 0.6 shard_map.74
  31.3 1.6 %collective-permute-start.5 = (bf16[2,64,512]{2,1,0:T(8,128)(2,1)S(1)}, bf16[2,64,512]{2,1,0:T(8,128)(2,1)S(1)}, u32[]{:S(2)}, u32[]{:S(2)}) collective-permute-start(bf16[2,64,512]{2,1,0:T(8,128)(2,1)S(1)} %get-tuple-element.40), channel_id=1, source_target_pairs={{0,2},{1,3},{2,0},{3,1},{4,6},{5,7},{6,4},{7,5},{8,10},{9,11},{10,... | collective-permute-start | bytes 393224 | tf_op jit(solution)/shard_map/ppermute | solution.py:154
  32.9 2.6 %collective-permute-start.6 = (bf16[2,64,512]{2,1,0:T(8,128)(2,1)S(1)}, bf16[2,64,512]{2,1,0:T(8,128)(2,1)S(1)}, u32[]{:S(2)}, u32[]{:S(2)}) collective-permute-start(bf16[2,64,512]{2,1,0:T(8,128)(2,1)S(1)} %get-tuple-element.41), channel_id=1, source_target_pairs={{0,4},{1,5},{2,6},{3,7},{4,0},{5,1},{6,2},{7,3},{8,12},{9,13},{10,... | collective-permute-start | bytes 393224 | tf_op jit(solution)/shard_map/ppermute | solution.py:154
  35.7 1.6 %copy-done.4 = f32[1,1,2,512,512]{4,3,2,1,0:T(8,128)S(1)} copy-done((f32[1,1,2,512,512]{4,3,2,1,0:T(8,128)S(1)}, f32[1,1,2,512,512]{4,3,2,1,0:T(8,128)}, u32[]{:S(2)}) %copy-start.4) | copy-done | bytes 2097176
  37.6 1.2 %collective-permute-done.5.refs_1_ = bf16[2,64,512]{2,1,0:T(8,128)(2,1)S(1)} collective-permute-done((bf16[2,64,512]{2,1,0:T(8,128)(2,1)S(1)}, bf16[2,64,512]{2,1,0:T(8,128)(2,1)S(1)}, u32[]{:S(2)}, u32[]{:S(2)}) %collective-permute-start.5) | collective-permute-done | bytes 131104 | tf_op jit(solution)/shard_map/ppermute | solution.py:154
  38.8 7.0 %collective-permute-done.6.refs_2_ = bf16[2,64,512]{2,1,0:T(8,128)(2,1)S(1)} collective-permute-done((bf16[2,64,512]{2,1,0:T(8,128)(2,1)S(1)}, bf16[2,64,512]{2,1,0:T(8,128)(2,1)S(1)}, u32[]{:S(2)}, u32[]{:S(2)}) %collective-permute-start.6) | collective-permute-done | bytes 131104 | tf_op jit(solution)/shard_map/ppermute | solution.py:154
  45.8 7.8 %shard_map.75 = (bf16[2,64,512]{2,1,0:T(8,128)(2,1)S(1)}, bf16[2,64,512]{2,1,0:T(8,128)(2,1)S(1)}, bf16[2,64,512]{2,1,0:T(8,128)(2,1)S(1)}, bf16[2,64,512]{2,1,0...) custom-call(s32[35]{0:T(128)S(1)} %concatenate.4.scal, f32[2,512,512]{2,1,0:T(8,128)S(1)} %get-tuple-element.33.l_ref, ...), custom_call_target="tpu_custom_call" | custom-call | flops 5368709120 | bytes 4718732 | tf_op jit(solution)/shard_map/pallas_call | solution.py:35
  53.8 4.3 %collective-permute-start.10 = (bf16[2,64,512]{2,1,0:T(8,128)(2,1)S(1)}, bf16[2,64,512]{2,1,0:T(8,128)(2,1)S(1)}, u32[]{:S(2)}, u32[]{:S(2)}) collective-permute-start(bf16[2,64,512]{2,1,0:T(8,128)(2,1)S(1)} %get-tuple-element.46), channel_id=1, source_target_pairs={{0,6},{1,7},{2,4},{3,5},{4,2},{5,3},{6,0},{7,1},{8,14},{9,15},{10,... | collective-permute-start | bytes 393224 | tf_op jit(solution)/shard_map/ppermute | solution.py:154
  58.8 3.7 %collective-permute-start.14 = (bf16[2,64,512]{2,1,0:T(8,128)(2,1)S(1)}, bf16[2,64,512]{2,1,0:T(8,128)(2,1)S(1)}, u32[]{:S(2)}, u32[]{:S(2)}) collective-permute-start(bf16[2,64,512]{2,1,0:T(8,128)(2,1)S(1)} %get-tuple-element.50), channel_id=1, source_target_pairs={{0,6},{1,7},{2,4},{3,5},{4,2},{5,3},{6,0},{7,1},{8,14},{9,15},{10,... | collective-permute-start | bytes 393224 | tf_op jit(solution)/shard_map/ppermute | solution.py:154
  62.5 5.5 %collective-permute-done.9.refs_2_ = bf16[2,64,512]{2,1,0:T(8,128)(2,1)S(1)} collective-permute-done((bf16[2,64,512]{2,1,0:T(8,128)(2,1)S(1)}, bf16[2,64,512]{2,1,0:T(8,128)(2,1)S(1)}, u32[]{:S(2)}, u32[]{:S(2)}) %collective-permute-start.9) | collective-permute-done | bytes 131104 | tf_op jit(solution)/shard_map/ppermute | solution.py:154
  68.7 9.0 %collective-permute-done.13.refs_2_ = bf16[2,64,512]{2,1,0:T(8,128)(2,1)S(1)} collective-permute-done((bf16[2,64,512]{2,1,0:T(8,128)(2,1)S(1)}, bf16[2,64,512]{2,1,0:T(8,128)(2,1)S(1)}, u32[]{:S(2)}, u32[]{:S(2)}) %collective-permute-start.13) | collective-permute-done | bytes 131104 | tf_op jit(solution)/shard_map/ppermute | solution.py:154
  77.7 8.0 %shard_map.77 = (bf16[64,512]{1,0:T(8,128)(2,1)S(1)}, bf16[64,512]{1,0:T(8,128)(2,1)S(1)}, bf16[64,512]{1,0:T(8,128)(2,1)S(1)}, bf16[64,512]{1,0:T(8,128)(2,1)S(...) custom-call(s32[35]{0:T(128)S(1)} %concatenate.4.scal, ...), custom_call_target="tpu_custom_call", output_to_operand_aliasing={{8}: (7, {}), {9}: (8, {})} | custom-call | flops 5368709120 | bytes 8913036 | tf_op jit(solution)/shard_map/pallas_call | solution.py:35
  85.9 3.4 %collective-permute-start.16 = (bf16[64,512]{1,0:T(8,128)(2,1)S(1)}, bf16[64,512]{1,0:T(8,128)(2,1)S(1)}, u32[]{:S(2)}, u32[]{:S(2)}) collective-permute-start(bf16[64,512]{1,0:T(8,128)(2,1)S(1)} %get-tuple-element.55), channel_id=1, source_target_pairs={{0,2},{1,3},{2,0},{3,1},{4,6},{5,7},{6,4},{7,5},{8,10},{9,11},{10,... | collective-permute-start | bytes 196616 | tf_op jit(solution)/shard_map/ppermute | solution.py:154
  89.3 2.4 %collective-permute-start.19 = (bf16[64,512]{1,0:T(8,128)(2,1)S(1)}, bf16[64,512]{1,0:T(8,128)(2,1)S(1)}, u32[]{:S(2)}, u32[]{:S(2)}) collective-permute-start(bf16[64,512]{1,0:T(8,128)(2,1)S(1)} %get-tuple-element.58), channel_id=1, source_target_pairs={{0,5},{1,4},{2,7},{3,6},{4,1},{5,0},{6,3},{7,2},{8,13},{9,12},{10,... | collective-permute-start | bytes 196616 | tf_op jit(solution)/shard_map/ppermute | solution.py:154
  91.7 1.6 %collective-permute-start.20 = (bf16[64,512]{1,0:T(8,128)(2,1)S(1)}, bf16[64,512]{1,0:T(8,128)(2,1)S(1)}, u32[]{:S(2)}, u32[]{:S(2)}) collective-permute-start(bf16[64,512]{1,0:T(8,128)(2,1)S(1)} %get-tuple-element.59), channel_id=1, source_target_pairs={{0,6},{1,7},{2,4},{3,5},{4,2},{5,3},{6,0},{7,1},{8,14},{9,15},{10,... | collective-permute-start | bytes 196616 | tf_op jit(solution)/shard_map/ppermute | solution.py:154
  93.4 1.8 %collective-permute-done.17.refs_8_ = bf16[64,512]{1,0:T(8,128)(2,1)S(1)} collective-permute-done((bf16[64,512]{1,0:T(8,128)(2,1)S(1)}, bf16[64,512]{1,0:T(8,128)(2,1)S(1)}, u32[]{:S(2)}, u32[]{:S(2)}) %collective-permute-start.17) | collective-permute-done | bytes 65568 | tf_op jit(solution)/shard_map/ppermute | solution.py:154
  95.5 3.9 %collective-permute-done.18.refs_9_ = bf16[64,512]{1,0:T(8,128)(2,1)S(1)} collective-permute-done((bf16[64,512]{1,0:T(8,128)(2,1)S(1)}, bf16[64,512]{1,0:T(8,128)(2,1)S(1)}, u32[]{:S(2)}, u32[]{:S(2)}) %collective-permute-start.18) | collective-permute-done | bytes 65568 | tf_op jit(solution)/shard_map/ppermute | solution.py:154
  99.4 1.8 %collective-permute-done.21.refs_12_ = bf16[64,512]{1,0:T(8,128)(2,1)S(1)} collective-permute-done((bf16[64,512]{1,0:T(8,128)(2,1)S(1)}, bf16[64,512]{1,0:T(8,128)(2,1)S(1)}, u32[]{:S(2)}, u32[]{:S(2)}) %collective-permute-start.21) | collective-permute-done | bytes 65568 | tf_op jit(solution)/shard_map/ppermute | solution.py:154
  101.2 1.5 %shard_map.78 = bf16[8,64,512]{2,1,0:T(8,128)(2,1)} custom-call(s32[35]{0:T(128)S(1)} %concatenate.4.scal, bf16[2,64,512]{2,1,0:T(8,128)(2,1)S(1)} %get-tuple-element.43.refs_0_, bf16[2,64,512]{2,1,0:T(8,128)(2,1)S(1)} %collective-permute-done.8.refs_1_, bf16[2,64,512]{2,1,0:T(8,128)(2,1)S(1)} %collective-permute-done.9.refs_2_, ...), custom_call_target="tpu_custom_call" | custom-call | bytes 1310860 | tf_op jit(solution)/shard_map/pallas_call | solution.py:35
  (43 shorter events, 4.6 us)
Async XLA Ops:
  0.6 22.5 %copy-start = (s32[4,8]{1,0:T(4,128)S(1)}, s32[4,8]{1,0:T(4,128)}, u32[]{:S(2)}) copy-start(s32[4,8]{1,0:T(4,128)} %param.5) | copy-start | bytes 388
  0.7 2.2 %copy-start.1 = (f32[1,4,8,64,512]{4,3,2,1,0:T(8,128)S(1)}, f32[1,4,8,64,512]{4,3,2,1,0:T(8,128)}, u32[]{:S(2)}) copy-start(f32[1,4,8,64,512]{4,3,2,1,0:T(8,128)} %param.4) | copy-start | bytes 12582916
  3.6 15.0 %collective-permute-start = (bf16[2,8,64,256]{3,2,1,0:T(8,128)(2,1)S(1)}, bf16[2,8,64,256]{3,2,1,0:T(8,128)(2,1)S(1)}, u32[]{:S(2)}, u32[]{:S(2)}) collective-permute-start(bf16[2,8,64,256]{3,2,1,0:T(8,128)(2,1)S(1)} %get-tuple-element.35), channel_id=1, source_target_pairs={{0,8},{8,0},{16,24},{24,16},{1,9},{9,1},{17,25},{25,17},{2,10},{10... | collective-permute-start | bytes 1572872 | tf_op jit(solution)/shard_map/ppermute | solution.py:90
  6.6 14.4 %collective-permute-start.1 = (bf16[2,8,64,256]{3,2,1,0:T(8,128)(2,1)S(1)}, bf16[2,8,64,256]{3,2,1,0:T(8,128)(2,1)S(1)}, u32[]{:S(2)}, u32[]{:S(2)}) collective-permute-start(bf16[2,8,64,256]{3,2,1,0:T(8,128)(2,1)S(1)} %get-tuple-element.36), channel_id=1, source_target_pairs={{0,16},{8,24},{16,0},{24,8},{1,17},{9,25},{17,1},{25,9},{2,18},{10... | collective-permute-start | bytes 1572872 | tf_op jit(solution)/shard_map/ppermute | solution.py:90
  19.2 7.5 %collective-permute-start.2 = (bf16[8,64,256]{2,1,0:T(8,128)(2,1)S(1)}, bf16[8,64,256]{2,1,0:T(8,128)(2,1)S(1)}, u32[]{:S(2)}, u32[]{:S(2)}) collective-permute-start(bf16[8,64,256]{2,1,0:T(8,128)(2,1)S(1)} %shard_map.71), channel_id=1, source_target_pairs={{0,16},{8,24},{16,0},{24,8},{1,17},{9,25},{17,1},{25,9},{2,18},{10... | collective-permute-start | bytes 786440 | tf_op jit(solution)/shard_map/ppermute | solution.py:98
  21.6 7.0 %collective-permute-start.3 = (bf16[8,64,256]{2,1,0:T(8,128)(2,1)S(1)}, bf16[8,64,256]{2,1,0:T(8,128)(2,1)S(1)}, u32[]{:S(2)}, u32[]{:S(2)}) collective-permute-start(bf16[8,64,256]{2,1,0:T(8,128)(2,1)S(1)} %shard_map.72), channel_id=1, source_target_pairs={{0,8},{8,0},{16,24},{24,16},{1,9},{9,1},{17,25},{25,17},{2,10},{10... | collective-permute-start | bytes 786440 | tf_op jit(solution)/shard_map/ppermute | solution.py:98
  23.3 2.2 %copy-start.2 = (f32[1,4,8,64,512]{4,3,2,1,0:T(8,128)S(1)}, f32[1,4,8,64,512]{4,3,2,1,0:T(8,128)}, u32[]{:S(2)}) copy-start(f32[1,4,8,64,512]{4,3,2,1,0:T(8,128)} %param.4) | copy-start | bytes 12582916
  26.1 9.7 %copy-start.3 = (f32[1,1,2,512,512]{4,3,2,1,0:T(8,128)S(1)}, f32[1,1,2,512,512]{4,3,2,1,0:T(8,128)}, u32[]{:S(2)}) copy-start(f32[1,1,2,512,512]{4,3,2,1,0:T(8,128)} %param.6) | copy-start | bytes 6291460
  28.7 2.0 %collective-permute-start.4 = (bf16[8,64,512]{2,1,0:T(8,128)(2,1)S(1)}, bf16[8,64,512]{2,1,0:T(8,128)(2,1)S(1)}, u32[]{:S(2)}, u32[]{:S(2)}) collective-permute-start(bf16[8,64,512]{2,1,0:T(8,128)(2,1)S(1)} %shard_map.73.own_ref), channel_id=1, source_target_pairs={{0,1},{1,0},{2,3},{3,2},{4,5},{5,4},{6,7},{7,6},{8,9},{9,8},{10,11... | collective-permute-start | bytes 1572872 | tf_op jit(solution)/shard_map/ppermute | solution.py:389
  31.3 7.5 %collective-permute-start.5 = (bf16[2,64,512]{2,1,0:T(8,128)(2,1)S(1)}, bf16[2,64,512]{2,1,0:T(8,128)(2,1)S(1)}, u32[]{:S(2)}, u32[]{:S(2)}) collective-permute-start(bf16[2,64,512]{2,1,0:T(8,128)(2,1)S(1)} %get-tuple-element.40), channel_id=1, source_target_pairs={{0,2},{1,3},{2,0},{3,1},{4,6},{5,7},{6,4},{7,5},{8,10},{9,11},{10,... | collective-permute-start | bytes 393224 | tf_op jit(solution)/shard_map/ppermute | solution.py:154
  32.9 12.9 %collective-permute-start.6 = (bf16[2,64,512]{2,1,0:T(8,128)(2,1)S(1)}, bf16[2,64,512]{2,1,0:T(8,128)(2,1)S(1)}, u32[]{:S(2)}, u32[]{:S(2)}) collective-permute-start(bf16[2,64,512]{2,1,0:T(8,128)(2,1)S(1)} %get-tuple-element.41), channel_id=1, source_target_pairs={{0,4},{1,5},{2,6},{3,7},{4,0},{5,1},{6,2},{7,3},{8,12},{9,13},{10,... | collective-permute-start | bytes 393224 | tf_op jit(solution)/shard_map/ppermute | solution.py:154
  35.5 10.3 %collective-permute-start.7 = (bf16[2,64,512]{2,1,0:T(8,128)(2,1)S(1)}, bf16[2,64,512]{2,1,0:T(8,128)(2,1)S(1)}, u32[]{:S(2)}, u32[]{:S(2)}) collective-permute-start(bf16[2,64,512]{2,1,0:T(8,128)(2,1)S(1)} %get-tuple-element.42), channel_id=1, source_target_pairs={{0,6},{1,7},{2,4},{3,5},{4,2},{5,3},{6,0},{7,1},{8,14},{9,15},{10,... | collective-permute-start | bytes 393224 | tf_op jit(solution)/shard_map/ppermute | solution.py:154
  35.7 1.6 %copy-start.4 = (f32[1,1,2,512,512]{4,3,2,1,0:T(8,128)S(1)}, f32[1,1,2,512,512]{4,3,2,1,0:T(8,128)}, u32[]{:S(2)}) copy-start(f32[1,1,2,512,512]{4,3,2,1,0:T(8,128)} %param.7) | copy-start | bytes 6291460
  53.6 5.1 %collective-permute-start.8 = (bf16[2,64,512]{2,1,0:T(8,128)(2,1)S(1)}, bf16[2,64,512]{2,1,0:T(8,128)(2,1)S(1)}, u32[]{:S(2)}, u32[]{:S(2)}) collective-permute-start(bf16[2,64,512]{2,1,0:T(8,128)(2,1)S(1)} %get-tuple-element.44), channel_id=1, source_target_pairs={{0,2},{1,3},{2,0},{3,1},{4,6},{5,7},{6,4},{7,5},{8,10},{9,11},{10,... | collective-permute-start | bytes 393224 | tf_op jit(solution)/shard_map/ppermute | solution.py:154
  53.7 14.3 %collective-permute-start.9 = (bf16[2,64,512]{2,1,0:T(8,128)(2,1)S(1)}, bf16[2,64,512]{2,1,0:T(8,128)(2,1)S(1)}, u32[]{:S(2)}, u32[]{:S(2)}) collective-permute-start(bf16[2,64,512]{2,1,0:T(8,128)(2,1)S(1)} %get-tuple-element.45), channel_id=1, source_target_pairs={{0,4},{1,5},{2,6},{3,7},{4,0},{5,1},{6,2},{7,3},{8,12},{9,13},{10,... | collective-permute-start | bytes 393224 | tf_op jit(solution)/shard_map/ppermute | solution.py:154
  53.8 14.2 %collective-permute-start.10 = (bf16[2,64,512]{2,1,0:T(8,128)(2,1)S(1)}, bf16[2,64,512]{2,1,0:T(8,128)(2,1)S(1)}, u32[]{:S(2)}, u32[]{:S(2)}) collective-permute-start(bf16[2,64,512]{2,1,0:T(8,128)(2,1)S(1)} %get-tuple-element.46), channel_id=1, source_target_pairs={{0,6},{1,7},{2,4},{3,5},{4,2},{5,3},{6,0},{7,1},{8,14},{9,15},{10,... | collective-permute-start | bytes 393224 | tf_op jit(solution)/shard_map/ppermute | solution.py:154
  58.1 10.7 %collective-permute-start.12 = (bf16[2,64,512]{2,1,0:T(8,128)(2,1)S(1)}, bf16[2,64,512]{2,1,0:T(8,128)(2,1)S(1)}, u32[]{:S(2)}, u32[]{:S(2)}) collective-permute-start(bf16[2,64,512]{2,1,0:T(8,128)(2,1)S(1)} %get-tuple-element.48), channel_id=1, source_target_pairs={{0,2},{1,3},{2,0},{3,1},{4,6},{5,7},{6,4},{7,5},{8,10},{9,11},{10,... | collective-permute-start | bytes 393224 | tf_op jit(solution)/shard_map/ppermute | solution.py:154
  58.1 19.6 %collective-permute-start.13 = (bf16[2,64,512]{2,1,0:T(8,128)(2,1)S(1)}, bf16[2,64,512]{2,1,0:T(8,128)(2,1)S(1)}, u32[]{:S(2)}, u32[]{:S(2)}) collective-permute-start(bf16[2,64,512]{2,1,0:T(8,128)(2,1)S(1)} %get-tuple-element.49), channel_id=1, source_target_pairs={{0,4},{1,5},{2,6},{3,7},{4,0},{5,1},{6,2},{7,3},{8,12},{9,13},{10,... | collective-permute-start | bytes 393224 | tf_op jit(solution)/shard_map/ppermute | solution.py:154
  58.8 19.0 %collective-permute-start.14 = (bf16[2,64,512]{2,1,0:T(8,128)(2,1)S(1)}, bf16[2,64,512]{2,1,0:T(8,128)(2,1)S(1)}, u32[]{:S(2)}, u32[]{:S(2)}) collective-permute-start(bf16[2,64,512]{2,1,0:T(8,128)(2,1)S(1)} %get-tuple-element.50), channel_id=1, source_target_pairs={{0,6},{1,7},{2,4},{3,5},{4,2},{5,3},{6,0},{7,1},{8,14},{9,15},{10,... | collective-permute-start | bytes 393224 | tf_op jit(solution)/shard_map/ppermute | solution.py:154
  68.6 32.6 %collective-permute-start.11 = (bf16[4,64,512]{2,1,0:T(8,128)(2,1)S(1)}, bf16[4,64,512]{2,1,0:T(8,128)(2,1)S(1)}, u32[]{:S(2)}, u32[]{:S(2)}) collective-permute-start(bf16[4,64,512]{2,1,0:T(8,128)(2,1)S(1)} %shard_map.76), channel_id=1, source_target_pairs={{0,1},{1,0},{2,3},{3,2},{4,5},{5,4},{6,7},{7,6},{8,9},{9,8},{10,11... | collective-permute-start | bytes 786440 | tf_op jit(solution)/shard_map/ppermute | solution.py:416
  85.7 3.6 %collective-permute-start.15 = (bf16[64,512]{1,0:T(8,128)(2,1)S(1)}, bf16[64,512]{1,0:T(8,128)(2,1)S(1)}, u32[]{:S(2)}, u32[]{:S(2)}) collective-permute-start(bf16[64,512]{1,0:T(8,128)(2,1)S(1)} %get-tuple-element.54), channel_id=1, source_target_pairs={{0,1},{1,0},{2,3},{3,2},{4,5},{5,4},{6,7},{7,6},{8,9},{9,8},{10,11... | collective-permute-start | bytes 196616 | tf_op jit(solution)/shard_map/ppermute | solution.py:154
  85.9 5.9 %collective-permute-start.16 = (bf16[64,512]{1,0:T(8,128)(2,1)S(1)}, bf16[64,512]{1,0:T(8,128)(2,1)S(1)}, u32[]{:S(2)}, u32[]{:S(2)}) collective-permute-start(bf16[64,512]{1,0:T(8,128)(2,1)S(1)} %get-tuple-element.55), channel_id=1, source_target_pairs={{0,2},{1,3},{2,0},{3,1},{4,6},{5,7},{6,4},{7,5},{8,10},{9,11},{10,... | collective-permute-start | bytes 196616 | tf_op jit(solution)/shard_map/ppermute | solution.py:154
  89.3 5.9 %collective-permute-start.17 = (bf16[64,512]{1,0:T(8,128)(2,1)S(1)}, bf16[64,512]{1,0:T(8,128)(2,1)S(1)}, u32[]{:S(2)}, u32[]{:S(2)}) collective-permute-start(bf16[64,512]{1,0:T(8,128)(2,1)S(1)} %get-tuple-element.56), channel_id=1, source_target_pairs={{0,3},{1,2},{2,1},{3,0},{4,7},{5,6},{6,5},{7,4},{8,11},{9,10},{10,... | collective-permute-start | bytes 196616 | tf_op jit(solution)/shard_map/ppermute | solution.py:154
  89.3 10.1 %collective-permute-start.18 = (bf16[64,512]{1,0:T(8,128)(2,1)S(1)}, bf16[64,512]{1,0:T(8,128)(2,1)S(1)}, u32[]{:S(2)}, u32[]{:S(2)}) collective-permute-start(bf16[64,512]{1,0:T(8,128)(2,1)S(1)} %get-tuple-element.57), channel_id=1, source_target_pairs={{0,4},{1,5},{2,6},{3,7},{4,0},{5,1},{6,2},{7,3},{8,12},{9,13},{10,... | collective-permute-start | bytes 196616 | tf_op jit(solution)/shard_map/ppermute | solution.py:154
  89.3 10.1 %collective-permute-start.19 = (bf16[64,512]{1,0:T(8,128)(2,1)S(1)}, bf16[64,512]{1,0:T(8,128)(2,1)S(1)}, u32[]{:S(2)}, u32[]{:S(2)}) collective-permute-start(bf16[64,512]{1,0:T(8,128)(2,1)S(1)} %get-tuple-element.58), channel_id=1, source_target_pairs={{0,5},{1,4},{2,7},{3,6},{4,1},{5,0},{6,3},{7,2},{8,13},{9,12},{10,... | collective-permute-start | bytes 196616 | tf_op jit(solution)/shard_map/ppermute | solution.py:154
  91.7 7.6 %collective-permute-start.20 = (bf16[64,512]{1,0:T(8,128)(2,1)S(1)}, bf16[64,512]{1,0:T(8,128)(2,1)S(1)}, u32[]{:S(2)}, u32[]{:S(2)}) collective-permute-start(bf16[64,512]{1,0:T(8,128)(2,1)S(1)} %get-tuple-element.59), channel_id=1, source_target_pairs={{0,6},{1,7},{2,4},{3,5},{4,2},{5,3},{6,0},{7,1},{8,14},{9,15},{10,... | collective-permute-start | bytes 196616 | tf_op jit(solution)/shard_map/ppermute | solution.py:154
  95.1 6.0 %collective-permute-start.21 = (bf16[64,512]{1,0:T(8,128)(2,1)S(1)}, bf16[64,512]{1,0:T(8,128)(2,1)S(1)}, u32[]{:S(2)}, u32[]{:S(2)}) collective-permute-start(bf16[64,512]{1,0:T(8,128)(2,1)S(1)} %get-tuple-element.60), channel_id=1, source_target_pairs={{0,7},{1,6},{2,5},{3,4},{4,3},{5,2},{6,1},{7,0},{8,15},{9,14},{10,... | collective-permute-start | bytes 196616 | tf_op jit(solution)/shard_map/ppermute | solution.py:154

commit v3 on v2

--- a/solution.py
+++ b/solution.py
@@ -44,36 +44,33 @@
     )(*[array for array, _ in operands])
 
 
-def cast_kernel(scal, p_ref, a_ref, b_ref):
-    cut = a_ref.shape[-1]
+def keep_kernel(scal, p_ref, a_ref, b_ref):
+    cut = a_ref.shape[0]
     high, low = scal[0], scal[1]
-    for other in range(2):
-        a_ref[other] = p_ref[other, 1 - low, :, :, :cut].astype(bf16)
-        b_ref[other] = p_ref[1 - high, other, :, :, cut:].astype(bf16)
-
-
-def keep_kernel(scal, p_ref, a_ref, b_ref):
-    cut = a_ref.shape[-1]
-    high, low = scal[0], scal[1]
-    a_ref[...] = p_ref[1 - high, low, :, :, :cut]
-    b_ref[...] = p_ref[high, 1 - low, :, :, cut:]
-
-
-def half_kernel(scal, p_ref, a1_ref, b1_ref, own_ref):
-    cut = a1_ref.shape[-1]
-    high, low = scal[0], scal[1]
-    own_ref[:, :, :cut] = p_ref[high, low, :, :, :cut] + a1_ref[high].astype(f32)
-    own_ref[:, :, cut:] = p_ref[high, low, :, :, cut:] + b1_ref[low].astype(f32)
+    a_ref[...] = p_ref[1 - high, low, :cut]
+    b_ref[...] = p_ref[high, 1 - low, cut:]
 
 
 def forward_kernel(bit, scal, kept_ref, first_ref, out_ref):
     out_ref[...] = (kept_ref[...] + first_ref[1 - scal[bit]].astype(f32)).astype(bf16)
 
 
-def total_kernel(own_ref, a2_ref, b2_ref, out_ref):
-    cut = a2_ref.shape[-1]
-    out_ref[:, :, :cut] = (own_ref[:, :, :cut] + a2_ref[...].astype(f32)).astype(bf16)
-    out_ref[:, :, cut:] = (own_ref[:, :, cut:] + b2_ref[...].astype(f32)).astype(bf16)
+def half_kernel(scal, p_ref, *refs):
+    *first_refs, own_ref = refs
+    blocks = first_refs[0].shape[1]
+    high, low = scal[0], scal[1]
+    for index, ref in enumerate(first_refs):
+        part = pl.ds(index * blocks, blocks)
+        bit = 2 * index // len(first_refs)
+        own_ref[part] = p_ref[high, low, part] + ref[(high, low)[bit]].astype(f32)
+
+
+def total_kernel(own_ref, *refs):
+    *second_refs, out_ref = refs
+    blocks = second_refs[0].shape[0]
+    for index, ref in enumerate(second_refs):
+        part = pl.ds(index * blocks, blocks)
+        out_ref[part] = (own_ref[part] + ref[...].astype(f32)).astype(bf16)
 
 
 def sum_over_dp(grad_partial, scal):
@@ -81,22 +78,28 @@
     p = grad_partial.reshape(2, rows // 2, count, stripe, size)
     over_low = [(i, i ^ 1) for i in range(rows)]
     over_high = [(i, i ^ 2) for i in range(rows)]
-    shape = (count, stripe, size // 2)
-    pair = (jax.ShapeDtypeStruct((2,) + shape, bf16), VMEM)
+    cut = count // 2
+    shape = (cut, stripe, size)
     one = (jax.ShapeDtypeStruct(shape, bf16), VMEM)
     both = (jax.ShapeDtypeStruct((count, stripe, size), bf16), VMEM)
+    high, low = scal[0], scal[1]
+    a = lax.dynamic_slice(p, (0, 1 - low, 0, 0, 0), (2, 1) + shape).reshape((2,) + shape)
+    b = lax.dynamic_slice(p, (1 - high, 0, cut, 0, 0), (1, 2) + shape).reshape((2,) + shape)
+    first = [
+        lax.ppermute(a.astype(bf16), "dp", over_low),
+        lax.ppermute(b.astype(bf16), "dp", over_high),
+    ]
     fixed = [(scal, SMEM), (p, VMEM)]
-    a, b = call(cast_kernel, [pair] * 2, [], fixed)
-    first = [lax.ppermute(a, "dp", over_low), lax.ppermute(b, "dp", over_high)]
     kept = [(jax.ShapeDtypeStruct(shape, f32), VMEM)] * 2
-    pa, pb = call(keep_kernel, kept, [], fixed)
-    arrived = [(array, VMEM) for array in first]
+    kept = call(keep_kernel, kept, [], fixed)
     second = []
-    for bit, (kept, perm) in enumerate([(pa, over_high), (pb, over_low)]):
-        operands = [(scal, SMEM), (kept, VMEM), (first[bit], VMEM)]
-        (summed,) = call(functools.partial(forward_kernel, bit), [one], [], operands)
+    for bit, perm in enumerate([over_high, over_low]):
+        operands = [(scal, SMEM), (kept[bit], VMEM), (first[bit], VMEM)]
+        kernel = functools.partial(forward_kernel, bit)
+        (summed,) = call(kernel, [one], [], operands)
         second.append(lax.ppermute(summed, "dp", perm))
     whole = [(jax.ShapeDtypeStruct((count, stripe, size), f32), VMEM)]
+    arrived = [(array, VMEM) for array in first]
     (own,) = call(half_kernel, whole, [], fixed + arrived)
     operands = [(own, VMEM)] + [(array, VMEM) for array in second]
     (total,) = call(total_kernel, [both], [], operands)

time: 103 us -> 102 us (level)
  local copies, waits for them, and re-layouts: 6.23 us -> 8.82 us
  waiting for transfers between devices: 44.1 us -> 41.6 us
    ppermute x2, waiting for transfers between devices: 9.78 us -> 6.85 us  [the longest x1 6.16 us: sum_over_dp(): lax.ppermute(a.astype(bf16), 'dp', over_low)]
    convert_element_type x0 -> x2, local copies, waits for them, and re-layouts: none -> 2.59 us  [the longest x1 1.3 us: sum_over_dp(): a.astype(bf16)]
    pallas_call x12 -> x11, Pallas kernels: 22 us -> 21.3 us  [call(): pl.pallas_call(kernel, in_specs=[pl.BlockSpec(memory_space=space) for _,...]
  transfers between devices with their start and end apart: 22 -> 22, of which waited for: 13 -> 14; matrix products, arithmetic and copies ran while one was open for 0% -> 2% of each run, Pallas kernels for 11% -> 11%
where the time goes in v3:
time: 102 us; the launch traced here: 101 us
  waiting for transfers between devices  41.6 us (41%)
  starting transfers between devices  28.6 us (28%)
  Pallas kernels  21.3 us (21%)
  local copies, waits for them, and re-layouts  8.82 us (9%)
    ppermute x16, waiting for transfers between devices, over_block(): moved.append(lax.ppermute(arrays[r], 'block', pairs))  30.4 us
    pallas_call x11, Pallas kernels, call(): pl.pallas_call(kernel, in_specs=[pl.BlockSpec(memory_space=space) for _,...  21.3 us
    ppermute x16, starting transfers between devices, over_block(): moved.append(lax.ppermute(arrays[r], 'block', pairs))  21 us
    ppermute x1, waiting for transfers between devices, sum_over_dp(): lax.ppermute(a.astype(bf16), 'dp', over_low)  6.16 us
    unnamed x10, local copies, waits for them, and re-layouts  5.98 us
    ppermute x1, starting transfers between devices, sum_over_dp(): lax.ppermute(a.astype(bf16), 'dp', over_low)  3.03 us
    ppermute x2, waiting for transfers between devices, sum_over_dp(): second.append(lax.ppermute(summed, 'dp', perm))  2.87 us
    ppermute x2, starting transfers between devices, sum_over_dp(): second.append(lax.ppermute(summed, 'dp', perm))  2.7 us
  transfers between devices with their start and end apart: 22, of which 14 were waited for; matrix products, arithmetic and copies ran while one was open for 2% of the time, Pallas kernels for 11%

profile of v3, /device:TPU:0, one launch (start us, length us, event | category | flops | bytes accessed | tf_op | source)
XLA Modules:
  0.0 101.5 jit_solution(7268111591921475682)
XLA Ops:
  0.7 1.3 %fusion = bf16[2,4,64,512]{3,2,1,0:T(8,128)(2,1)S(1)} fusion(f32[2,2,8,64,512]{4,3,2,1,0:T(8,128)} %bitcast.15, s32[]{:T(128)S(6)} %select_n.29), kind=kLoop, calls=%fused_computation.2 | loop fusion | bytes 1048580 | tf_op jit(solution)/shard_map/convert_element_type | solution.py:89
  2.0 3.0 %collective-permute-start = (bf16[2,4,64,512]{3,2,1,0:T(8,128)(2,1)S(1)}, bf16[2,4,64,512]{3,2,1,0:T(8,128)(2,1)S(1)}, u32[]{:S(2)}, u32[]{:S(2)}) collective-permute-start(bf16[2,4,64,512]{3,2,1,0:T(8,128)(2,1)S(1)} %fusion), channel_id=1, source_target_pairs={{0,8},{8,0},{16,24},{24,16},{1,9},{9,1},{17,25},{25,17},{2,10},{10... | collective-permute-start | bytes 1572872 | tf_op jit(solution)/shard_map/ppermute | solution.py:89
  5.0 1.3 %fusion.1 = bf16[2,4,64,512]{3,2,1,0:T(8,128)(2,1)S(1)} fusion(f32[2,2,8,64,512]{4,3,2,1,0:T(8,128)} %bitcast.16, s32[]{:T(128)S(6)} %select_n.30), kind=kLoop, calls=%fused_computation.3 | loop fusion | bytes 1048580 | tf_op jit(solution)/shard_map/convert_element_type | solution.py:90
  6.3 1.6 %collective-permute-start.1 = (bf16[2,4,64,512]{3,2,1,0:T(8,128)(2,1)S(1)}, bf16[2,4,64,512]{3,2,1,0:T(8,128)(2,1)S(1)}, u32[]{:S(2)}, u32[]{:S(2)}) collective-permute-start(bf16[2,4,64,512]{3,2,1,0:T(8,128)(2,1)S(1)} %fusion.1), channel_id=1, source_target_pairs={{0,16},{8,24},{16,0},{24,8},{1,17},{9,25},{17,1},{25,9},{2,18},{10... | collective-permute-start | bytes 1572872 | tf_op jit(solution)/shard_map/ppermute | solution.py:90
  8.0 2.2 %copy-done.1 = f32[1,4,8,64,512]{4,3,2,1,0:T(8,128)S(1)} copy-done((f32[1,4,8,64,512]{4,3,2,1,0:T(8,128)S(1)}, f32[1,4,8,64,512]{4,3,2,1,0:T(8,128)}, u32[]{:S(2)}) %copy-start.1) | copy-done | bytes 4194328
  10.8 6.2 %collective-permute-done.refs_0_.first_ref = bf16[2,4,64,512]{3,2,1,0:T(8,128)(2,1)S(1)} collective-permute-done((bf16[2,4,64,512]{3,2,1,0:T(8,128)(2,1)S(1)}, bf16[2,4,64,512]{3,2,1,0:T(8,128)(2,1)S(1)}, u32[]{:S(2)}, u32[]{:S(2)}) %collective-permute-start) | collective-permute-done | bytes 524320 | tf_op jit(solution)/shard_map/ppermute | solution.py:89
  17.5 1.8 %collective-permute-start.2 = (bf16[4,64,512]{2,1,0:T(8,128)(2,1)S(1)}, bf16[4,64,512]{2,1,0:T(8,128)(2,1)S(1)}, u32[]{:S(2)}, u32[]{:S(2)}) collective-permute-start(bf16[4,64,512]{2,1,0:T(8,128)(2,1)S(1)} %shard_map.70), channel_id=1, source_target_pairs={{0,16},{8,24},{16,0},{24,8},{1,17},{9,25},{17,1},{25,9},{2,18},{10... | collective-permute-start | bytes 786440 | tf_op jit(solution)/shard_map/ppermute | solution.py:100
  19.4 0.7 collective-permute-done.1.refs_1_.first_ref
  20.6 0.9 collective-permute-start.3
  21.6 2.2 %copy-done.2 = f32[1,4,8,64,512]{4,3,2,1,0:T(8,128)S(1)} copy-done((f32[1,4,8,64,512]{4,3,2,1,0:T(8,128)S(1)}, f32[1,4,8,64,512]{4,3,2,1,0:T(8,128)}, u32[]{:S(2)}) %copy-start.2) | copy-done | bytes 4194328
  23.8 0.6 shard_map.68.own_ref
  24.4 0.9 collective-permute-done.2.refs_0_
  25.4 2.0 %collective-permute-done.3.refs_1_ = bf16[4,64,512]{2,1,0:T(8,128)(2,1)S(1)} collective-permute-done((bf16[4,64,512]{2,1,0:T(8,128)(2,1)S(1)}, bf16[4,64,512]{2,1,0:T(8,128)(2,1)S(1)}, u32[]{:S(2)}, u32[]{:S(2)}) %collective-permute-start.3) | collective-permute-done | bytes 262176 | tf_op jit(solution)/shard_map/ppermute | solution.py:100
  27.9 1.5 %collective-permute-done.4.other_ref = bf16[8,64,512]{2,1,0:T(8,128)(2,1)S(1)} collective-permute-done((bf16[8,64,512]{2,1,0:T(8,128)(2,1)S(1)}, bf16[8,64,512]{2,1,0:T(8,128)(2,1)S(1)}, u32[]{:S(2)}, u32[]{:S(2)}) %collective-permute-start.4) | collective-permute-done | bytes 524320 | tf_op jit(solution)/shard_map/ppermute | solution.py:392
  30.0 1.6 %collective-permute-start.5 = (bf16[2,64,512]{2,1,0:T(8,128)(2,1)S(1)}, bf16[2,64,512]{2,1,0:T(8,128)(2,1)S(1)}, u32[]{:S(2)}, u32[]{:S(2)}) collective-permute-start(bf16[2,64,512]{2,1,0:T(8,128)(2,1)S(1)} %get-tuple-element.36), channel_id=1, source_target_pairs={{0,2},{1,3},{2,0},{3,1},{4,6},{5,7},{6,4},{7,5},{8,10},{9,11},{10,... | collective-permute-start | bytes 393224 | tf_op jit(solution)/shard_map/ppermute | solution.py:157
  31.7 2.6 %collective-permute-start.6 = (bf16[2,64,512]{2,1,0:T(8,128)(2,1)S(1)}, bf16[2,64,512]{2,1,0:T(8,128)(2,1)S(1)}, u32[]{:S(2)}, u32[]{:S(2)}) collective-permute-start(bf16[2,64,512]{2,1,0:T(8,128)(2,1)S(1)} %get-tuple-element.37), channel_id=1, source_target_pairs={{0,4},{1,5},{2,6},{3,7},{4,0},{5,1},{6,2},{7,3},{8,12},{9,13},{10,... | collective-permute-start | bytes 393224 | tf_op jit(solution)/shard_map/ppermute | solution.py:157
  34.5 1.6 %copy-done.4 = f32[1,1,2,512,512]{4,3,2,1,0:T(8,128)S(1)} copy-done((f32[1,1,2,512,512]{4,3,2,1,0:T(8,128)S(1)}, f32[1,1,2,512,512]{4,3,2,1,0:T(8,128)}, u32[]{:S(2)}) %copy-start.4) | copy-done | bytes 2097176
  36.3 1.2 %collective-permute-done.5.refs_1_ = bf16[2,64,512]{2,1,0:T(8,128)(2,1)S(1)} collective-permute-done((bf16[2,64,512]{2,1,0:T(8,128)(2,1)S(1)}, bf16[2,64,512]{2,1,0:T(8,128)(2,1)S(1)}, u32[]{:S(2)}, u32[]{:S(2)}) %collective-permute-start.5) | collective-permute-done | bytes 131104 | tf_op jit(solution)/shard_map/ppermute | solution.py:157
  37.6 7.0 %collective-permute-done.6.refs_2_ = bf16[2,64,512]{2,1,0:T(8,128)(2,1)S(1)} collective-permute-done((bf16[2,64,512]{2,1,0:T(8,128)(2,1)S(1)}, bf16[2,64,512]{2,1,0:T(8,128)(2,1)S(1)}, u32[]{:S(2)}, u32[]{:S(2)}) %collective-permute-start.6) | collective-permute-done | bytes 131104 | tf_op jit(solution)/shard_map/ppermute | solution.py:157
  44.5 7.8 %shard_map.74 = (bf16[2,64,512]{2,1,0:T(8,128)(2,1)S(1)}, bf16[2,64,512]{2,1,0:T(8,128)(2,1)S(1)}, bf16[2,64,512]{2,1,0:T(8,128)(2,1)S(1)}, bf16[2,64,512]{2,1,0...) custom-call(s32[35]{0:T(128)S(1)} %concatenate.4.scal, f32[2,512,512]{2,1,0:T(8,128)S(1)} %get-tuple-element.31.l_ref, ...), custom_call_target="tpu_custom_call" | custom-call | flops 5368709120 | bytes 4718732 | tf_op jit(solution)/shard_map/pallas_call | solution.py:35
  52.5 4.3 %collective-permute-start.10 = (bf16[2,64,512]{2,1,0:T(8,128)(2,1)S(1)}, bf16[2,64,512]{2,1,0:T(8,128)(2,1)S(1)}, u32[]{:S(2)}, u32[]{:S(2)}) collective-permute-start(bf16[2,64,512]{2,1,0:T(8,128)(2,1)S(1)} %get-tuple-element.42), channel_id=1, source_target_pairs={{0,6},{1,7},{2,4},{3,5},{4,2},{5,3},{6,0},{7,1},{8,14},{9,15},{10,... | collective-permute-start | bytes 393224 | tf_op jit(solution)/shard_map/ppermute | solution.py:157
  57.5 3.7 %collective-permute-start.14 = (bf16[2,64,512]{2,1,0:T(8,128)(2,1)S(1)}, bf16[2,64,512]{2,1,0:T(8,128)(2,1)S(1)}, u32[]{:S(2)}, u32[]{:S(2)}) collective-permute-start(bf16[2,64,512]{2,1,0:T(8,128)(2,1)S(1)} %get-tuple-element.46), channel_id=1, source_target_pairs={{0,6},{1,7},{2,4},{3,5},{4,2},{5,3},{6,0},{7,1},{8,14},{9,15},{10,... | collective-permute-start | bytes 393224 | tf_op jit(solution)/shard_map/ppermute | solution.py:157
  61.2 5.5 %collective-permute-done.9.refs_2_ = bf16[2,64,512]{2,1,0:T(8,128)(2,1)S(1)} collective-permute-done((bf16[2,64,512]{2,1,0:T(8,128)(2,1)S(1)}, bf16[2,64,512]{2,1,0:T(8,128)(2,1)S(1)}, u32[]{:S(2)}, u32[]{:S(2)}) %collective-permute-start.9) | collective-permute-done | bytes 131104 | tf_op jit(solution)/shard_map/ppermute | solution.py:157
  67.5 9.0 %collective-permute-done.13.refs_2_ = bf16[2,64,512]{2,1,0:T(8,128)(2,1)S(1)} collective-permute-done((bf16[2,64,512]{2,1,0:T(8,128)(2,1)S(1)}, bf16[2,64,512]{2,1,0:T(8,128)(2,1)S(1)}, u32[]{:S(2)}, u32[]{:S(2)}) %collective-permute-start.13) | collective-permute-done | bytes 131104 | tf_op jit(solution)/shard_map/ppermute | solution.py:157
  76.5 8.0 %shard_map.76 = (bf16[64,512]{1,0:T(8,128)(2,1)S(1)}, bf16[64,512]{1,0:T(8,128)(2,1)S(1)}, bf16[64,512]{1,0:T(8,128)(2,1)S(1)}, bf16[64,512]{1,0:T(8,128)(2,1)S(...) custom-call(s32[35]{0:T(128)S(1)} %concatenate.4.scal, ...), custom_call_target="tpu_custom_call", output_to_operand_aliasing={{8}: (7, {}), {9}: (8, {})} | custom-call | flops 5368709120 | bytes 8913036 | tf_op jit(solution)/shard_map/pallas_call | solution.py:35
  84.7 3.4 %collective-permute-start.16 = (bf16[64,512]{1,0:T(8,128)(2,1)S(1)}, bf16[64,512]{1,0:T(8,128)(2,1)S(1)}, u32[]{:S(2)}, u32[]{:S(2)}) collective-permute-start(bf16[64,512]{1,0:T(8,128)(2,1)S(1)} %get-tuple-element.51), channel_id=1, source_target_pairs={{0,2},{1,3},{2,0},{3,1},{4,6},{5,7},{6,4},{7,5},{8,10},{9,11},{10,... | collective-permute-start | bytes 196616 | tf_op jit(solution)/shard_map/ppermute | solution.py:157
  88.1 2.4 %collective-permute-start.19 = (bf16[64,512]{1,0:T(8,128)(2,1)S(1)}, bf16[64,512]{1,0:T(8,128)(2,1)S(1)}, u32[]{:S(2)}, u32[]{:S(2)}) collective-permute-start(bf16[64,512]{1,0:T(8,128)(2,1)S(1)} %get-tuple-element.54), channel_id=1, source_target_pairs={{0,5},{1,4},{2,7},{3,6},{4,1},{5,0},{6,3},{7,2},{8,13},{9,12},{10,... | collective-permute-start | bytes 196616 | tf_op jit(solution)/shard_map/ppermute | solution.py:157
  90.5 1.6 %collective-permute-start.20 = (bf16[64,512]{1,0:T(8,128)(2,1)S(1)}, bf16[64,512]{1,0:T(8,128)(2,1)S(1)}, u32[]{:S(2)}, u32[]{:S(2)}) collective-permute-start(bf16[64,512]{1,0:T(8,128)(2,1)S(1)} %get-tuple-element.55), channel_id=1, source_target_pairs={{0,6},{1,7},{2,4},{3,5},{4,2},{5,3},{6,0},{7,1},{8,14},{9,15},{10,... | collective-permute-start | bytes 196616 | tf_op jit(solution)/shard_map/ppermute | solution.py:157
  92.2 1.8 %collective-permute-done.17.refs_8_ = bf16[64,512]{1,0:T(8,128)(2,1)S(1)} collective-permute-done((bf16[64,512]{1,0:T(8,128)(2,1)S(1)}, bf16[64,512]{1,0:T(8,128)(2,1)S(1)}, u32[]{:S(2)}, u32[]{:S(2)}) %collective-permute-start.17) | collective-permute-done | bytes 65568 | tf_op jit(solution)/shard_map/ppermute | solution.py:157
  94.2 3.9 %collective-permute-done.18.refs_9_ = bf16[64,512]{1,0:T(8,128)(2,1)S(1)} collective-permute-done((bf16[64,512]{1,0:T(8,128)(2,1)S(1)}, bf16[64,512]{1,0:T(8,128)(2,1)S(1)}, u32[]{:S(2)}, u32[]{:S(2)}) %collective-permute-start.18) | collective-permute-done | bytes 65568 | tf_op jit(solution)/shard_map/ppermute | solution.py:157
  98.2 1.8 %collective-permute-done.21.refs_12_ = bf16[64,512]{1,0:T(8,128)(2,1)S(1)} collective-permute-done((bf16[64,512]{1,0:T(8,128)(2,1)S(1)}, bf16[64,512]{1,0:T(8,128)(2,1)S(1)}, u32[]{:S(2)}, u32[]{:S(2)}) %collective-permute-start.21) | collective-permute-done | bytes 65568 | tf_op jit(solution)/shard_map/ppermute | solution.py:157
  100.0 1.5 %shard_map.77 = bf16[8,64,512]{2,1,0:T(8,128)(2,1)} custom-call(s32[35]{0:T(128)S(1)} %concatenate.4.scal, bf16[2,64,512]{2,1,0:T(8,128)(2,1)S(1)} %get-tuple-element.39.refs_0_, bf16[2,64,512]{2,1,0:T(8,128)(2,1)S(1)} %collective-permute-done.8.refs_1_, bf16[2,64,512]{2,1,0:T(8,128)(2,1)S(1)} %collective-permute-done.9.refs_2_, ...), custom_call_target="tpu_custom_call" | custom-call | bytes 1310860 | tf_op jit(solution)/shard_map/pallas_call | solution.py:35
  (44 shorter events, 5.9 us)
Async XLA Ops:
  0.6 20.9 %copy-start = (s32[4,8]{1,0:T(4,128)S(1)}, s32[4,8]{1,0:T(4,128)}, u32[]{:S(2)}) copy-start(s32[4,8]{1,0:T(4,128)} %param.5) | copy-start | bytes 388
  2.0 15.0 %collective-permute-start = (bf16[2,4,64,512]{3,2,1,0:T(8,128)(2,1)S(1)}, bf16[2,4,64,512]{3,2,1,0:T(8,128)(2,1)S(1)}, u32[]{:S(2)}, u32[]{:S(2)}) collective-permute-start(bf16[2,4,64,512]{3,2,1,0:T(8,128)(2,1)S(1)} %fusion), channel_id=1, source_target_pairs={{0,8},{8,0},{16,24},{24,16},{1,9},{9,1},{17,25},{25,17},{2,10},{10... | collective-permute-start | bytes 1572872 | tf_op jit(solution)/shard_map/ppermute | solution.py:89
  6.3 13.8 %collective-permute-start.1 = (bf16[2,4,64,512]{3,2,1,0:T(8,128)(2,1)S(1)}, bf16[2,4,64,512]{3,2,1,0:T(8,128)(2,1)S(1)}, u32[]{:S(2)}, u32[]{:S(2)}) collective-permute-start(bf16[2,4,64,512]{3,2,1,0:T(8,128)(2,1)S(1)} %fusion.1), channel_id=1, source_target_pairs={{0,16},{8,24},{16,0},{24,8},{1,17},{9,25},{17,1},{25,9},{2,18},{10... | collective-permute-start | bytes 1572872 | tf_op jit(solution)/shard_map/ppermute | solution.py:90
  8.0 2.2 %copy-start.1 = (f32[1,4,8,64,512]{4,3,2,1,0:T(8,128)S(1)}, f32[1,4,8,64,512]{4,3,2,1,0:T(8,128)}, u32[]{:S(2)}) copy-start(f32[1,4,8,64,512]{4,3,2,1,0:T(8,128)} %param.4) | copy-start | bytes 12582916
  17.5 7.8 %collective-permute-start.2 = (bf16[4,64,512]{2,1,0:T(8,128)(2,1)S(1)}, bf16[4,64,512]{2,1,0:T(8,128)(2,1)S(1)}, u32[]{:S(2)}, u32[]{:S(2)}) collective-permute-start(bf16[4,64,512]{2,1,0:T(8,128)(2,1)S(1)} %shard_map.70), channel_id=1, source_target_pairs={{0,16},{8,24},{16,0},{24,8},{1,17},{9,25},{17,1},{25,9},{2,18},{10... | collective-permute-start | bytes 786440 | tf_op jit(solution)/shard_map/ppermute | solution.py:100
  20.6 6.7 %collective-permute-start.3 = (bf16[4,64,512]{2,1,0:T(8,128)(2,1)S(1)}, bf16[4,64,512]{2,1,0:T(8,128)(2,1)S(1)}, u32[]{:S(2)}, u32[]{:S(2)}) collective-permute-start(bf16[4,64,512]{2,1,0:T(8,128)(2,1)S(1)} %shard_map.71), channel_id=1, source_target_pairs={{0,8},{8,0},{16,24},{24,16},{1,9},{9,1},{17,25},{25,17},{2,10},{10... | collective-permute-start | bytes 786440 | tf_op jit(solution)/shard_map/ppermute | solution.py:100
  21.6 2.2 %copy-start.2 = (f32[1,4,8,64,512]{4,3,2,1,0:T(8,128)S(1)}, f32[1,4,8,64,512]{4,3,2,1,0:T(8,128)}, u32[]{:S(2)}) copy-start(f32[1,4,8,64,512]{4,3,2,1,0:T(8,128)} %param.4) | copy-start | bytes 12582916
  24.4 10.0 %copy-start.3 = (f32[1,1,2,512,512]{4,3,2,1,0:T(8,128)S(1)}, f32[1,1,2,512,512]{4,3,2,1,0:T(8,128)}, u32[]{:S(2)}) copy-start(f32[1,1,2,512,512]{4,3,2,1,0:T(8,128)} %param.6) | copy-start | bytes 6291460
  27.4 2.0 %collective-permute-start.4 = (bf16[8,64,512]{2,1,0:T(8,128)(2,1)S(1)}, bf16[8,64,512]{2,1,0:T(8,128)(2,1)S(1)}, u32[]{:S(2)}, u32[]{:S(2)}) collective-permute-start(bf16[8,64,512]{2,1,0:T(8,128)(2,1)S(1)} %shard_map.72.own_ref), channel_id=1, source_target_pairs={{0,1},{1,0},{2,3},{3,2},{4,5},{5,4},{6,7},{7,6},{8,9},{9,8},{10,11... | collective-permute-start | bytes 1572872 | tf_op jit(solution)/shard_map/ppermute | solution.py:392
  30.0 7.5 %collective-permute-start.5 = (bf16[2,64,512]{2,1,0:T(8,128)(2,1)S(1)}, bf16[2,64,512]{2,1,0:T(8,128)(2,1)S(1)}, u32[]{:S(2)}, u32[]{:S(2)}) collective-permute-start(bf16[2,64,512]{2,1,0:T(8,128)(2,1)S(1)} %get-tuple-element.36), channel_id=1, source_target_pairs={{0,2},{1,3},{2,0},{3,1},{4,6},{5,7},{6,4},{7,5},{8,10},{9,11},{10,... | collective-permute-start | bytes 393224 | tf_op jit(solution)/shard_map/ppermute | solution.py:157
  31.7 12.9 %collective-permute-start.6 = (bf16[2,64,512]{2,1,0:T(8,128)(2,1)S(1)}, bf16[2,64,512]{2,1,0:T(8,128)(2,1)S(1)}, u32[]{:S(2)}, u32[]{:S(2)}) collective-permute-start(bf16[2,64,512]{2,1,0:T(8,128)(2,1)S(1)} %get-tuple-element.37), channel_id=1, source_target_pairs={{0,4},{1,5},{2,6},{3,7},{4,0},{5,1},{6,2},{7,3},{8,12},{9,13},{10,... | collective-permute-start | bytes 393224 | tf_op jit(solution)/shard_map/ppermute | solution.py:157
  34.2 10.3 %collective-permute-start.7 = (bf16[2,64,512]{2,1,0:T(8,128)(2,1)S(1)}, bf16[2,64,512]{2,1,0:T(8,128)(2,1)S(1)}, u32[]{:S(2)}, u32[]{:S(2)}) collective-permute-start(bf16[2,64,512]{2,1,0:T(8,128)(2,1)S(1)} %get-tuple-element.38), channel_id=1, source_target_pairs={{0,6},{1,7},{2,4},{3,5},{4,2},{5,3},{6,0},{7,1},{8,14},{9,15},{10,... | collective-permute-start | bytes 393224 | tf_op jit(solution)/shard_map/ppermute | solution.py:157
  34.5 1.6 %copy-start.4 = (f32[1,1,2,512,512]{4,3,2,1,0:T(8,128)S(1)}, f32[1,1,2,512,512]{4,3,2,1,0:T(8,128)}, u32[]{:S(2)}) copy-start(f32[1,1,2,512,512]{4,3,2,1,0:T(8,128)} %param.7) | copy-start | bytes 6291460
  52.4 5.1 %collective-permute-start.8 = (bf16[2,64,512]{2,1,0:T(8,128)(2,1)S(1)}, bf16[2,64,512]{2,1,0:T(8,128)(2,1)S(1)}, u32[]{:S(2)}, u32[]{:S(2)}) collective-permute-start(bf16[2,64,512]{2,1,0:T(8,128)(2,1)S(1)} %get-tuple-element.40), channel_id=1, source_target_pairs={{0,2},{1,3},{2,0},{3,1},{4,6},{5,7},{6,4},{7,5},{8,10},{9,11},{10,... | collective-permute-start | bytes 393224 | tf_op jit(solution)/shard_map/ppermute | solution.py:157
  52.5 14.3 %collective-permute-start.9 = (bf16[2,64,512]{2,1,0:T(8,128)(2,1)S(1)}, bf16[2,64,512]{2,1,0:T(8,128)(2,1)S(1)}, u32[]{:S(2)}, u32[]{:S(2)}) collective-permute-start(bf16[2,64,512]{2,1,0:T(8,128)(2,1)S(1)} %get-tuple-element.41), channel_id=1, source_target_pairs={{0,4},{1,5},{2,6},{3,7},{4,0},{5,1},{6,2},{7,3},{8,12},{9,13},{10,... | collective-permute-start | bytes 393224 | tf_op jit(solution)/shard_map/ppermute | solution.py:157
  52.5 14.2 %collective-permute-start.10 = (bf16[2,64,512]{2,1,0:T(8,128)(2,1)S(1)}, bf16[2,64,512]{2,1,0:T(8,128)(2,1)S(1)}, u32[]{:S(2)}, u32[]{:S(2)}) collective-permute-start(bf16[2,64,512]{2,1,0:T(8,128)(2,1)S(1)} %get-tuple-element.42), channel_id=1, source_target_pairs={{0,6},{1,7},{2,4},{3,5},{4,2},{5,3},{6,0},{7,1},{8,14},{9,15},{10,... | collective-permute-start | bytes 393224 | tf_op jit(solution)/shard_map/ppermute | solution.py:157
  56.8 10.7 %collective-permute-start.12 = (bf16[2,64,512]{2,1,0:T(8,128)(2,1)S(1)}, bf16[2,64,512]{2,1,0:T(8,128)(2,1)S(1)}, u32[]{:S(2)}, u32[]{:S(2)}) collective-permute-start(bf16[2,64,512]{2,1,0:T(8,128)(2,1)S(1)} %get-tuple-element.44), channel_id=1, source_target_pairs={{0,2},{1,3},{2,0},{3,1},{4,6},{5,7},{6,4},{7,5},{8,10},{9,11},{10,... | collective-permute-start | bytes 393224 | tf_op jit(solution)/shard_map/ppermute | solution.py:157
  56.8 19.6 %collective-permute-start.13 = (bf16[2,64,512]{2,1,0:T(8,128)(2,1)S(1)}, bf16[2,64,512]{2,1,0:T(8,128)(2,1)S(1)}, u32[]{:S(2)}, u32[]{:S(2)}) collective-permute-start(bf16[2,64,512]{2,1,0:T(8,128)(2,1)S(1)} %get-tuple-element.45), channel_id=1, source_target_pairs={{0,4},{1,5},{2,6},{3,7},{4,0},{5,1},{6,2},{7,3},{8,12},{9,13},{10,... | collective-permute-start | bytes 393224 | tf_op jit(solution)/shard_map/ppermute | solution.py:157
  57.5 19.0 %collective-permute-start.14 = (bf16[2,64,512]{2,1,0:T(8,128)(2,1)S(1)}, bf16[2,64,512]{2,1,0:T(8,128)(2,1)S(1)}, u32[]{:S(2)}, u32[]{:S(2)}) collective-permute-start(bf16[2,64,512]{2,1,0:T(8,128)(2,1)S(1)} %get-tuple-element.46), channel_id=1, source_target_pairs={{0,6},{1,7},{2,4},{3,5},{4,2},{5,3},{6,0},{7,1},{8,14},{9,15},{10,... | collective-permute-start | bytes 393224 | tf_op jit(solution)/shard_map/ppermute | solution.py:157
  67.3 32.6 %collective-permute-start.11 = (bf16[4,64,512]{2,1,0:T(8,128)(2,1)S(1)}, bf16[4,64,512]{2,1,0:T(8,128)(2,1)S(1)}, u32[]{:S(2)}, u32[]{:S(2)}) collective-permute-start(bf16[4,64,512]{2,1,0:T(8,128)(2,1)S(1)} %shard_map.75), channel_id=1, source_target_pairs={{0,1},{1,0},{2,3},{3,2},{4,5},{5,4},{6,7},{7,6},{8,9},{9,8},{10,11... | collective-permute-start | bytes 786440 | tf_op jit(solution)/shard_map/ppermute | solution.py:419
  84.5 3.6 %collective-permute-start.15 = (bf16[64,512]{1,0:T(8,128)(2,1)S(1)}, bf16[64,512]{1,0:T(8,128)(2,1)S(1)}, u32[]{:S(2)}, u32[]{:S(2)}) collective-permute-start(bf16[64,512]{1,0:T(8,128)(2,1)S(1)} %get-tuple-element.50), channel_id=1, source_target_pairs={{0,1},{1,0},{2,3},{3,2},{4,5},{5,4},{6,7},{7,6},{8,9},{9,8},{10,11... | collective-permute-start | bytes 196616 | tf_op jit(solution)/shard_map/ppermute | solution.py:157
  84.7 5.9 %collective-permute-start.16 = (bf16[64,512]{1,0:T(8,128)(2,1)S(1)}, bf16[64,512]{1,0:T(8,128)(2,1)S(1)}, u32[]{:S(2)}, u32[]{:S(2)}) collective-permute-start(bf16[64,512]{1,0:T(8,128)(2,1)S(1)} %get-tuple-element.51), channel_id=1, source_target_pairs={{0,2},{1,3},{2,0},{3,1},{4,6},{5,7},{6,4},{7,5},{8,10},{9,11},{10,... | collective-permute-start | bytes 196616 | tf_op jit(solution)/shard_map/ppermute | solution.py:157
  88.0 5.9 %collective-permute-start.17 = (bf16[64,512]{1,0:T(8,128)(2,1)S(1)}, bf16[64,512]{1,0:T(8,128)(2,1)S(1)}, u32[]{:S(2)}, u32[]{:S(2)}) collective-permute-start(bf16[64,512]{1,0:T(8,128)(2,1)S(1)} %get-tuple-element.52), channel_id=1, source_target_pairs={{0,3},{1,2},{2,1},{3,0},{4,7},{5,6},{6,5},{7,4},{8,11},{9,10},{10,... | collective-permute-start | bytes 196616 | tf_op jit(solution)/shard_map/ppermute | solution.py:157
  88.0 10.1 %collective-permute-start.18 = (bf16[64,512]{1,0:T(8,128)(2,1)S(1)}, bf16[64,512]{1,0:T(8,128)(2,1)S(1)}, u32[]{:S(2)}, u32[]{:S(2)}) collective-permute-start(bf16[64,512]{1,0:T(8,128)(2,1)S(1)} %get-tuple-element.53), channel_id=1, source_target_pairs={{0,4},{1,5},{2,6},{3,7},{4,0},{5,1},{6,2},{7,3},{8,12},{9,13},{10,... | collective-permute-start | bytes 196616 | tf_op jit(solution)/shard_map/ppermute | solution.py:157
  88.1 10.1 %collective-permute-start.19 = (bf16[64,512]{1,0:T(8,128)(2,1)S(1)}, bf16[64,512]{1,0:T(8,128)(2,1)S(1)}, u32[]{:S(2)}, u32[]{:S(2)}) collective-permute-start(bf16[64,512]{1,0:T(8,128)(2,1)S(1)} %get-tuple-element.54), channel_id=1, source_target_pairs={{0,5},{1,4},{2,7},{3,6},{4,1},{5,0},{6,3},{7,2},{8,13},{9,12},{10,... | collective-permute-start | bytes 196616 | tf_op jit(solution)/shard_map/ppermute | solution.py:157
  90.5 7.6 %collective-permute-start.20 = (bf16[64,512]{1,0:T(8,128)(2,1)S(1)}, bf16[64,512]{1,0:T(8,128)(2,1)S(1)}, u32[]{:S(2)}, u32[]{:S(2)}) collective-permute-start(bf16[64,512]{1,0:T(8,128)(2,1)S(1)} %get-tuple-element.55), channel_id=1, source_target_pairs={{0,6},{1,7},{2,4},{3,5},{4,2},{5,3},{6,0},{7,1},{8,14},{9,15},{10,... | collective-permute-start | bytes 196616 | tf_op jit(solution)/shard_map/ppermute | solution.py:157
  93.9 6.0 %collective-permute-start.21 = (bf16[64,512]{1,0:T(8,128)(2,1)S(1)}, bf16[64,512]{1,0:T(8,128)(2,1)S(1)}, u32[]{:S(2)}, u32[]{:S(2)}) collective-permute-start(bf16[64,512]{1,0:T(8,128)(2,1)S(1)} %get-tuple-element.56), channel_id=1, source_target_pairs={{0,7},{1,6},{2,5},{3,4},{4,3},{5,2},{6,1},{7,0},{8,15},{9,14},{10,... | collective-permute-start | bytes 196616 | tf_op jit(solution)/shard_map/ppermute | solution.py:157
